TPU v7x, 32 devices: a whole 2x2x4 slice. The times are simulated.
32 devices in a mesh: dp: 4 (over x, core), section: 2 (over y), mp: 4 (over z).
Axes of the slice: x: 2, y: 2, z: 4, core: 2. Of those that a mesh axis runs over, the one named last changes fastest.
Arguments:
- micro_inputs: bfloat16 [8, 64, 4096], P(('dp', 'section'), None, 'mp'), parts along dimension 0, may hold values from -6 to 6
- qkv_weight: bfloat16 [2, 4096, 3, 2048], P('section', None, None, 'mp'), may hold values from -0.09375 to 0.09375
- out_weight: bfloat16 [2, 2048, 4096], P('section', None, 'mp'), may hold values from -0.125 to 0.125
- norm_gain: bfloat16 [2, 4096], P('section'), may hold values from 0.099609375 to 1.8984375
- position_bias: float32 [32, 32], P('mp'), may hold values from -3 to 280
Outputs:
- encoded: bfloat16 [8, 64, 4096], P(('dp', 'section'), None, 'mp'), parts along dimension 0
There are 4 independent parts, one for each index of `dp`. A program takes and returns all parts, laid end to end along the dimension named above; an argument that names none is the same for every part. Nothing has to cross between parts.
All inputs are finite; a program needn't handle non-finite values.
Results may differ from a plain program's by a relative error of at most 0.025.
Values may be sent and summed in bfloat16 or wider, within the bound.
No kernel may reach another device: no remote copies, remote signals or barrier semaphores. Data moves between devices by JAX's collectives and lax.ppermute only.
A program may use at most 128 MiB of HBM per device.

v0:
```python
import math

import jax
import jax.numpy as jnp
import numpy as np
from jax import lax
from jax.sharding import PartitionSpec as P

REACH = 128


NORM_EPSILON = 0.1


def shifted(x, axis, by):
    peers = lax.axis_size(axis)
    pairs = [(i, i + by) for i in range(peers) if 0 <= i + by < peers]
    return lax.ppermute(x, axis, pairs)


def bucket_table(length, bucket_count, reach_limit):
    offset = np.arange(length)[None, :] - np.arange(length)[:, None]
    half_count = bucket_count // 2
    upper_side = (offset > 0).astype(np.int32) * half_count
    distance = np.abs(offset)
    exact_count = half_count // 2
    scaled = (
        np.log(np.maximum(distance, 1) / exact_count)
        / np.log(reach_limit / exact_count)
        * (half_count - exact_count)
    )
    far_bucket = np.minimum(exact_count + scaled.astype(np.int32), half_count - 1)
    return (upper_side + np.where(distance < exact_count, distance, far_bucket)).astype(np.int32)


def shards(micro_inputs, qkv_weight, out_weight, norm_gain, position_bias):
    sections = lax.axis_size("section")
    section_index = lax.axis_index("section")
    length = micro_inputs.shape[1]
    local_width = micro_inputs.shape[2]
    model_width = qkv_weight.shape[1]
    local_heads = position_bias.shape[0]
    head_size = qkv_weight.shape[3] // local_heads
    weights_qkv = qkv_weight[0].reshape(model_width, 3 * qkv_weight.shape[3])
    weights_out = out_weight[0]
    gain_row = norm_gain[0]
    bucket_count = position_bias.shape[1]
    bucket_grid = jnp.asarray(bucket_table(length, bucket_count, REACH))
    onehot = (
        bucket_grid[:, :, None] == jnp.arange(bucket_count, dtype=jnp.int32)[None, None, :]
    ).astype(jnp.float32)
    score_bias = jnp.einsum("hb,ijb->hij", position_bias, onehot, precision=lax.Precision.HIGHEST)
    score_scale = 1.0 / math.sqrt(head_size)

    def attend(section_in):
        stream = section_in.astype(jnp.float32)
        portion_rows = lax.all_gather(section_in, "mp", axis=1, tiled=True).astype(jnp.float32)
        gain_piece = gain_row.astype(jnp.float32)
        gained_piece = (portion_rows * gain_piece).astype(jnp.bfloat16)
        weight_block = weights_qkv
        running = jnp.dot(gained_piece, weight_block, preferred_element_type=jnp.float32)
        project = running
        squares = jnp.sum(portion_rows * portion_rows, axis=1)
        row_scale = lax.rsqrt(squares / model_width + NORM_EPSILON)[:, None]
        project = (
            (project * row_scale).astype(jnp.bfloat16).reshape(length, 3, local_heads, head_size)
        )
        queries = project[:, 0]
        key_heads = project[:, 1]
        values = project[:, 2]
        scores = (
            jnp.einsum("ihd,jhd->hij", queries, key_heads, preferred_element_type=jnp.float32)
            * score_scale
            + score_bias
        )
        row_max = jnp.max(scores, axis=2, keepdims=True)
        weights = jnp.exp(scores - row_max)
        attn_probs = (weights / jnp.sum(weights, axis=2, keepdims=True)).astype(jnp.bfloat16)
        head_mix = jnp.einsum(
            "hij,jhd->ihd", attn_probs, values, preferred_element_type=jnp.float32
        )
        head_mix = head_mix.astype(jnp.bfloat16).reshape(length, local_heads * head_size)
        weight_block = weights_out
        update = jnp.dot(
            lax.all_gather(head_mix, "mp", axis=1, tiled=True),
            weight_block,
            preferred_element_type=jnp.float32,
        )
        return (stream + update).astype(jnp.bfloat16)

    def forward_step(section_in):
        section_out = attend(section_in)
        return (section_out, shifted(section_out, "section", 1))

    ticks = 2 * sections - 1
    first_section = section_index == 0
    last_section = section_index == sections - 1
    blank = jnp.zeros((length, local_width), jnp.bfloat16)

    def conveyor_tick(tick_index, state_pair):
        belt, received = state_pair
        section_out, received = forward_step(jnp.where(first_section, belt[0], received))
        belt = shifted(belt, "section", -1)
        belt = belt.at[1].set(jnp.where(last_section, section_out, belt[1]))
        return (belt, received)

    belt_start = jnp.stack([micro_inputs[0], blank])
    final_pair = lax.fori_loop(0, ticks, conveyor_tick, (belt_start, blank))
    return final_pair[0][1][None]


def solution(mesh):
    in_specs = (
        P(("dp", "section"), None, "mp"),
        P("section", None, None, "mp"),
        P("section", None, "mp"),
        P("section", None),
        P("mp", None),
    )
    out_specs = P(("dp", "section"), None, "mp")
    return jax.shard_map(shards, mesh=mesh, in_specs=in_specs, out_specs=out_specs, check_vma=False)
```

profile of v0, /device:TPU:0, one launch (start us, length us, event | category | flops | bytes accessed | tf_op | source)
XLA Modules:
  0.0 187.1 jit_solution(15900364324202981719)
XLA Ops:
  0.0 17.0 %copy.17 = bf16[1,4096,3,512]{1,3,2,0:T(8,128)(2,1)} copy(bf16[1,4096,3,512]{3,1,2,0:T(8,128)(2,1)} %param.11) | data formatting | bytes 25165824 | tf_op args[1]
  17.0 16.6 %copy.18 = bf16[4096,1536]{1,0:T(8,128)(2,1)} copy(bf16[4096,1536]{0,1:T(8,128)(2,1)} %bitcast.63) | data formatting | bytes 25165824 | tf_op jit(solution)/shard_map/while | solution.py:108
  34.3 152.1 %while.15 = (s32[]{:T(128)}, bf16[2,64,1024]{2,1,0:T(8,128)(2,1)S(1)}, bf16[64,1024]{1,0:T(8,128)(2,1)S(1)}, pred[]{:T(512)}, pred[]{:T(512)}, /*index=5*/bf16[4...) while((s32[]{:T(128)}, ...), condition=%wide.region_4.0_spmd, body=%wide.region_0.4_spmd.sunk | while | flops 1084494592 | bytes 24294580 | solution.py:108
  34.4 1.3 collective-permute-start
  35.7 17.4 %all_gather.14 = bf16[64,4096]{1,0:T(8,128)(2,1)S(1)} all-gather(bf16[64,1024]{1,0:T(8,128)(2,1)S(1)} %bitcast_select_fusion.2), channel_id=1, replica_groups=mesh['dp'=4,'section'=2,'mp'=4] {'mp'}, dimensions={1}, use_global_device_ids=true | all-gather | bytes 655360 | tf_op jit(solution)/shard_map/while/body/eval_jaxpr/all_gather | solution.py:57
  53.3 6.8 %fusion.46 = bf16[64,1536]{1,0:T(8,128)(2,1)S(1)} fusion(bf16[4096,1536]{1,0:T(8,128)(2,1)} %get-tuple-element.264, bf16[64,4096]{1,0:T(8,128)(2,1)S(1)} %all_gather.14, f32[4096]{0:T(1024)S(1)} %convert_element_type.84, f32[64]{0:T(128)S(1)} %add_rsqrt_fusion.2), kind=kOutput, calls=%fused_computation.2.clone.1 | convolution fusion | flops 806289408 | bytes 13320448 | tf_op jit(solution)/shard_map/while/body/eval_jaxpr/dot_general | solution.py:61
  61.1 16.2 %all_gather.15 = bf16[64,2048]{0,1:T(8,128)(2,1)S(1)} all-gather(bf16[64,512]{0,1:T(8,128)(2,1)S(1)} %bitcast.64), channel_id=1, replica_groups=mesh['dp'=4,'section'=2,'mp'=4] {'mp'}, dimensions={1}, use_global_device_ids=true | all-gather | bytes 327680 | tf_op jit(solution)/shard_map/while/body/eval_jaxpr/all_gather | solution.py:85
  77.4 3.1 %fusion.50 = (bf16[2,64,1024]{2,1,0:T(8,128)(2,1)S(1)}, bf16[64,1024]{1,0:T(8,128)(2,1)S(1)}) fusion(bf16[2,64,1024]{2,1,0:T(8,128)(2,1)S(1)} %collective-permute-done, pred[]{:T(512)} %get-tuple-element.261, bf16[64,2048]{0,1:T(8,128)(2,1)S(1)} %all_gather.15, bf16[2048,1024]{1,0:T(8,128)(2,1)} %get-tuple-element.266, ...), kind=kOutput, calls=%fused_computation.19.clone.1 | convolution fusion | flops 268697600 | bytes 5242881 | tf_op jit(solution)/shard_map/while/body/eval_jaxpr/dot_general | solution.py:84
  80.4 4.3 %collective-permute-start.1 = (bf16[64,1024]{1,0:T(8,128)(2,1)S(1)}, bf16[64,1024]{1,0:T(8,128)(2,1)S(1)}, u32[]{:S(2)}, u32[]{:S(2)}) collective-permute-start(bf16[64,1024]{1,0:T(8,128)(2,1)S(1)} %get-tuple-element.237), channel_id=1, source_target_pairs={{0,4},{1,5},{2,6},{3,7},{8,12},{9,13},{10,14},{11,15},{16,20},{17,... | collective-permute-start | bytes 393224 | tf_op jit(solution)/shard_map/while/body/eval_jaxpr/ppermute | solution.py:18
  84.8 2.5 %collective-permute-done.1 = bf16[64,1024]{1,0:T(8,128)(2,1)S(1)} collective-permute-done((bf16[64,1024]{1,0:T(8,128)(2,1)S(1)}, bf16[64,1024]{1,0:T(8,128)(2,1)S(1)}, u32[]{:S(2)}, u32[]{:S(2)}) %collective-permute-start.1) | collective-permute-done | bytes 131104 | tf_op jit(solution)/shard_map/while/body/eval_jaxpr/ppermute | solution.py:18
  87.3 1.3 collective-permute-start
  88.6 15.1 %all_gather.14 = bf16[64,4096]{1,0:T(8,128)(2,1)S(1)} all-gather(bf16[64,1024]{1,0:T(8,128)(2,1)S(1)} %bitcast_select_fusion.2), channel_id=1, replica_groups=mesh['dp'=4,'section'=2,'mp'=4] {'mp'}, dimensions={1}, use_global_device_ids=true | all-gather | bytes 655360 | tf_op jit(solution)/shard_map/while/body/eval_jaxpr/all_gather | solution.py:57
  103.9 6.8 %fusion.46 = bf16[64,1536]{1,0:T(8,128)(2,1)S(1)} fusion(bf16[4096,1536]{1,0:T(8,128)(2,1)} %get-tuple-element.264, bf16[64,4096]{1,0:T(8,128)(2,1)S(1)} %all_gather.14, f32[4096]{0:T(1024)S(1)} %convert_element_type.84, f32[64]{0:T(128)S(1)} %add_rsqrt_fusion.2), kind=kOutput, calls=%fused_computation.2.clone.1 | convolution fusion | flops 806289408 | bytes 13320448 | tf_op jit(solution)/shard_map/while/body/eval_jaxpr/dot_general | solution.py:61
  111.7 14.9 %all_gather.15 = bf16[64,2048]{0,1:T(8,128)(2,1)S(1)} all-gather(bf16[64,512]{0,1:T(8,128)(2,1)S(1)} %bitcast.64), channel_id=1, replica_groups=mesh['dp'=4,'section'=2,'mp'=4] {'mp'}, dimensions={1}, use_global_device_ids=true | all-gather | bytes 327680 | tf_op jit(solution)/shard_map/while/body/eval_jaxpr/all_gather | solution.py:85
  126.7 3.1 %fusion.50 = (bf16[2,64,1024]{2,1,0:T(8,128)(2,1)S(1)}, bf16[64,1024]{1,0:T(8,128)(2,1)S(1)}) fusion(bf16[2,64,1024]{2,1,0:T(8,128)(2,1)S(1)} %collective-permute-done, pred[]{:T(512)} %get-tuple-element.261, bf16[64,2048]{0,1:T(8,128)(2,1)S(1)} %all_gather.15, bf16[2048,1024]{1,0:T(8,128)(2,1)} %get-tuple-element.266, ...), kind=kOutput, calls=%fused_computation.19.clone.1 | convolution fusion | flops 268697600 | bytes 5242881 | tf_op jit(solution)/shard_map/while/body/eval_jaxpr/dot_general | solution.py:84
  129.7 4.6 %collective-permute-start.1 = (bf16[64,1024]{1,0:T(8,128)(2,1)S(1)}, bf16[64,1024]{1,0:T(8,128)(2,1)S(1)}, u32[]{:S(2)}, u32[]{:S(2)}) collective-permute-start(bf16[64,1024]{1,0:T(8,128)(2,1)S(1)} %get-tuple-element.237), channel_id=1, source_target_pairs={{0,4},{1,5},{2,6},{3,7},{8,12},{9,13},{10,14},{11,15},{16,20},{17,... | collective-permute-start | bytes 393224 | tf_op jit(solution)/shard_map/while/body/eval_jaxpr/ppermute | solution.py:18
  134.3 2.5 %collective-permute-done.1 = bf16[64,1024]{1,0:T(8,128)(2,1)S(1)} collective-permute-done((bf16[64,1024]{1,0:T(8,128)(2,1)S(1)}, bf16[64,1024]{1,0:T(8,128)(2,1)S(1)}, u32[]{:S(2)}, u32[]{:S(2)}) %collective-permute-start.1) | collective-permute-done | bytes 131104 | tf_op jit(solution)/shard_map/while/body/eval_jaxpr/ppermute | solution.py:18
  136.8 1.3 collective-permute-start
  138.1 15.3 %all_gather.14 = bf16[64,4096]{1,0:T(8,128)(2,1)S(1)} all-gather(bf16[64,1024]{1,0:T(8,128)(2,1)S(1)} %bitcast_select_fusion.2), channel_id=1, replica_groups=mesh['dp'=4,'section'=2,'mp'=4] {'mp'}, dimensions={1}, use_global_device_ids=true | all-gather | bytes 655360 | tf_op jit(solution)/shard_map/while/body/eval_jaxpr/all_gather | solution.py:57
  153.7 6.8 %fusion.46 = bf16[64,1536]{1,0:T(8,128)(2,1)S(1)} fusion(bf16[4096,1536]{1,0:T(8,128)(2,1)} %get-tuple-element.264, bf16[64,4096]{1,0:T(8,128)(2,1)S(1)} %all_gather.14, f32[4096]{0:T(1024)S(1)} %convert_element_type.84, f32[64]{0:T(128)S(1)} %add_rsqrt_fusion.2), kind=kOutput, calls=%fused_computation.2.clone.1 | convolution fusion | flops 806289408 | bytes 13320448 | tf_op jit(solution)/shard_map/while/body/eval_jaxpr/dot_general | solution.py:61
  161.5 14.8 %all_gather.15 = bf16[64,2048]{0,1:T(8,128)(2,1)S(1)} all-gather(bf16[64,512]{0,1:T(8,128)(2,1)S(1)} %bitcast.64), channel_id=1, replica_groups=mesh['dp'=4,'section'=2,'mp'=4] {'mp'}, dimensions={1}, use_global_device_ids=true | all-gather | bytes 327680 | tf_op jit(solution)/shard_map/while/body/eval_jaxpr/all_gather | solution.py:85
  176.3 3.1 %fusion.50 = (bf16[2,64,1024]{2,1,0:T(8,128)(2,1)S(1)}, bf16[64,1024]{1,0:T(8,128)(2,1)S(1)}) fusion(bf16[2,64,1024]{2,1,0:T(8,128)(2,1)S(1)} %collective-permute-done, pred[]{:T(512)} %get-tuple-element.261, bf16[64,2048]{0,1:T(8,128)(2,1)S(1)} %all_gather.15, bf16[2048,1024]{1,0:T(8,128)(2,1)} %get-tuple-element.266, ...), kind=kOutput, calls=%fused_computation.19.clone.1 | convolution fusion | flops 268697600 | bytes 5242881 | tf_op jit(solution)/shard_map/while/body/eval_jaxpr/dot_general | solution.py:84
  179.3 4.7 %collective-permute-start.1 = (bf16[64,1024]{1,0:T(8,128)(2,1)S(1)}, bf16[64,1024]{1,0:T(8,128)(2,1)S(1)}, u32[]{:S(2)}, u32[]{:S(2)}) collective-permute-start(bf16[64,1024]{1,0:T(8,128)(2,1)S(1)} %get-tuple-element.237), channel_id=1, source_target_pairs={{0,4},{1,5},{2,6},{3,7},{8,12},{9,13},{10,14},{11,15},{16,20},{17,... | collective-permute-start | bytes 393224 | tf_op jit(solution)/shard_map/while/body/eval_jaxpr/ppermute | solution.py:18
  184.0 2.5 %collective-permute-done.1 = bf16[64,1024]{1,0:T(8,128)(2,1)S(1)} collective-permute-done((bf16[64,1024]{1,0:T(8,128)(2,1)S(1)}, bf16[64,1024]{1,0:T(8,128)(2,1)S(1)}, u32[]{:S(2)}, u32[]{:S(2)}) %collective-permute-start.1) | collective-permute-done | bytes 131104 | tf_op jit(solution)/shard_map/while/body/eval_jaxpr/ppermute | solution.py:18
  (50 shorter events, 5.0 us)
Async XLA Ops:
  0.0 33.6 %copy-start = (f32[8,32]{1,0:T(8,128)S(1)}, f32[8,32]{1,0:T(8,128)}, u32[]{:S(2)}) copy-start(f32[8,32]{1,0:T(8,128)} %param.14) | copy-start | bytes 3076
  17.0 16.7 %copy-start.2 = (s32[64,64]{1,0:T(8,128)S(1)}, s32[64,64]{1,0:T(8,128)}, u32[]{:S(2)}) copy-start(s32[64,64]{1,0:T(8,128)} %constant.94.clone) | copy-start | bytes 49156
  17.0 17.2 %copy-start.1 = (bf16[1,64,1024]{2,1,0:T(8,128)(2,1)S(1)}, bf16[1,64,1024]{2,1,0:T(8,128)(2,1)}, u32[]{:S(2)}) copy-start(bf16[1,64,1024]{2,1,0:T(8,128)(2,1)} %param.10) | copy-start | bytes 393220
  17.0 17.3 %copy-start.3 = (bf16[1,4096]{1,0:T(2,128)(2,1)S(1)}, bf16[1,4096]{1,0:T(2,128)(2,1)}, u32[]{:S(2)}) copy-start(bf16[1,4096]{1,0:T(2,128)(2,1)} %param.13) | copy-start | bytes 24580
  34.4 43.0 %collective-permute-start = (bf16[2,64,1024]{2,1,0:T(8,128)(2,1)S(1)}, bf16[2,64,1024]{2,1,0:T(8,128)(2,1)S(1)}, u32[]{:S(2)}, u32[]{:S(2)}) collective-permute-start(bf16[2,64,1024]{2,1,0:T(8,128)(2,1)S(1)} %get-tuple-element.249), channel_id=1, source_target_pairs={{4,0},{5,1},{6,2},{7,3},{12,8},{13,9},{14,10},{15,11},{20,16},{21,... | collective-permute-start | bytes 786440 | tf_op jit(solution)/shard_map/while/body/eval_jaxpr/ppermute | solution.py:18
  80.4 6.8 %collective-permute-start.1 = (bf16[64,1024]{1,0:T(8,128)(2,1)S(1)}, bf16[64,1024]{1,0:T(8,128)(2,1)S(1)}, u32[]{:S(2)}, u32[]{:S(2)}) collective-permute-start(bf16[64,1024]{1,0:T(8,128)(2,1)S(1)} %get-tuple-element.237), channel_id=1, source_target_pairs={{0,4},{1,5},{2,6},{3,7},{8,12},{9,13},{10,14},{11,15},{16,20},{17,... | collective-permute-start | bytes 393224 | tf_op jit(solution)/shard_map/while/body/eval_jaxpr/ppermute | solution.py:18
  87.3 39.4 %collective-permute-start = (bf16[2,64,1024]{2,1,0:T(8,128)(2,1)S(1)}, bf16[2,64,1024]{2,1,0:T(8,128)(2,1)S(1)}, u32[]{:S(2)}, u32[]{:S(2)}) collective-permute-start(bf16[2,64,1024]{2,1,0:T(8,128)(2,1)S(1)} %get-tuple-element.249), channel_id=1, source_target_pairs={{4,0},{5,1},{6,2},{7,3},{12,8},{13,9},{14,10},{15,11},{20,16},{21,... | collective-permute-start | bytes 786440 | tf_op jit(solution)/shard_map/while/body/eval_jaxpr/ppermute | solution.py:18
  129.7 7.1 %collective-permute-start.1 = (bf16[64,1024]{1,0:T(8,128)(2,1)S(1)}, bf16[64,1024]{1,0:T(8,128)(2,1)S(1)}, u32[]{:S(2)}, u32[]{:S(2)}) collective-permute-start(bf16[64,1024]{1,0:T(8,128)(2,1)S(1)} %get-tuple-element.237), channel_id=1, source_target_pairs={{0,4},{1,5},{2,6},{3,7},{8,12},{9,13},{10,14},{11,15},{16,20},{17,... | collective-permute-start | bytes 393224 | tf_op jit(solution)/shard_map/while/body/eval_jaxpr/ppermute | solution.py:18
  136.8 39.5 %collective-permute-start = (bf16[2,64,1024]{2,1,0:T(8,128)(2,1)S(1)}, bf16[2,64,1024]{2,1,0:T(8,128)(2,1)S(1)}, u32[]{:S(2)}, u32[]{:S(2)}) collective-permute-start(bf16[2,64,1024]{2,1,0:T(8,128)(2,1)S(1)} %get-tuple-element.249), channel_id=1, source_target_pairs={{4,0},{5,1},{6,2},{7,3},{12,8},{13,9},{14,10},{15,11},{20,16},{21,... | collective-permute-start | bytes 786440 | tf_op jit(solution)/shard_map/while/body/eval_jaxpr/ppermute | solution.py:18
  179.3 7.2 %collective-permute-start.1 = (bf16[64,1024]{1,0:T(8,128)(2,1)S(1)}, bf16[64,1024]{1,0:T(8,128)(2,1)S(1)}, u32[]{:S(2)}, u32[]{:S(2)}) collective-permute-start(bf16[64,1024]{1,0:T(8,128)(2,1)S(1)} %get-tuple-element.237), channel_id=1, source_target_pairs={{0,4},{1,5},{2,6},{3,7},{8,12},{9,13},{10,14},{11,15},{16,20},{17,... | collective-permute-start | bytes 393224 | tf_op jit(solution)/shard_map/while/body/eval_jaxpr/ppermute | solution.py:18
where the time goes:
time: 188 us; the launch traced here: 187 us
  blocking collectives  93.7 us (50%)
  local copies, waits for them, and re-layouts  35.9 us (19%)
  matrix products  31.3 us (17%)
  starting transfers between devices  17.4 us (9%)
  waiting for transfers between devices  7.42 us (4%)
    all_gather x3, blocking collectives, attend(): lax.all_gather(section_in, 'mp', axis=1, tiled=True).astype(jnp.float32)  47.8 us
    all_gather x3, blocking collectives, attend(): lax.all_gather(head_mix, 'mp', axis=1, tiled=True)  46 us
    dot_general x3, matrix products, attend(): jnp.dot(gained_piece, weight_block, preferred_element_type=jnp.float32)  20.5 us
    ppermute x6, starting transfers between devices, shifted(): return lax.ppermute(x, axis, pairs)  17.4 us
    unnamed x9, local copies, waits for them, and re-layouts  17 us
    while x2, local copies, waits for them, and re-layouts, shards(): final_pair = lax.fori_loop(0, ticks, conveyor_tick, (belt_start, blank))  16.8 us
    dot_general x3, matrix products, attend(): jnp.dot(lax.all_gather(head_mix, 'mp', axis=1, tiled=True), weight_block,...  9.19 us
    ppermute x6, waiting for transfers between devices, shifted(): return lax.ppermute(x, axis, pairs)  7.42 us
  transfers between devices with their start and end apart: 6, of which 3 were waited for; matrix products, arithmetic and copies ran while one was open for 13% of the time, Pallas kernels for 0%

commit v1 on v0

v1 whole, which is shorter than its diff:
```python
import math

import jax
import jax.numpy as jnp
import numpy as np
from jax import lax
from jax.sharding import PartitionSpec as P

REACH = 128
NORM_EPSILON = 0.1
MOST_DIRECT = 4


def bucket_table(length, bucket_count, reach_limit):
    offset = np.arange(length)[None, :] - np.arange(length)[:, None]
    half_count = bucket_count // 2
    upper_side = (offset > 0).astype(np.int32) * half_count
    distance = np.abs(offset)
    exact_count = half_count // 2
    scaled = (
        np.log(np.maximum(distance, 1) / exact_count)
        / np.log(reach_limit / exact_count)
        * (half_count - exact_count)
    )
    far_bucket = np.minimum(exact_count + scaled.astype(np.int32), half_count - 1)
    return (upper_side + np.where(distance < exact_count, distance, far_bucket)).astype(np.int32)


def swap_orders(peers):
    return sorted(range(1, peers), key=lambda mask: (bin(mask).count("1"), mask))


def pieces(x, axis):
    peers = lax.axis_size(axis)
    me = lax.axis_index(axis)
    if peers & (peers - 1) or peers > MOST_DIRECT:
        whole = lax.all_gather(x, axis, axis=0, tiled=False)
        return [(p, whole[p]) for p in range(peers)]
    got = [(me, x)]
    for mask in swap_orders(peers):
        other = lax.ppermute(x, axis, [(i, i ^ mask) for i in range(peers)])
        got.append((me ^ mask, other))
    return got


def shards(micro_inputs, qkv_weight, out_weight, norm_gain, position_bias):
    sections = lax.axis_size("section")
    section_index = lax.axis_index("section")
    length = micro_inputs.shape[1]
    local_width = micro_inputs.shape[2]
    model_width = qkv_weight.shape[1]
    local_heads = position_bias.shape[0]
    local_qkv = qkv_weight.shape[3]
    head_size = local_qkv // local_heads
    peers = lax.axis_size("mp")
    weights_qkv = jnp.transpose(qkv_weight[0], (1, 0, 2))
    weights_out = out_weight[0]
    gain_row = norm_gain[0].astype(jnp.float32)
    bucket_count = position_bias.shape[1]
    bucket_grid = jnp.asarray(bucket_table(length, bucket_count, REACH))
    onehot = (
        bucket_grid[:, :, None] == jnp.arange(bucket_count, dtype=jnp.int32)[None, None, :]
    ).astype(jnp.float32)
    score_bias = jnp.einsum("hb,ijb->hij", position_bias, onehot, precision=lax.Precision.HIGHEST)
    score_scale = 1.0 / math.sqrt(head_size)

    def attend(section_in):
        stream = section_in.astype(jnp.float32)
        project = jnp.zeros((3, length, local_qkv), jnp.float32)
        squares = jnp.zeros((length,), jnp.float32)
        for peer, block in pieces(section_in, "mp"):
            rows = block.astype(jnp.float32)
            squares = squares + jnp.sum(rows * rows, axis=1)
            start = peer * local_width
            gain = lax.dynamic_slice_in_dim(gain_row, start, local_width, 0)
            part = lax.dynamic_slice_in_dim(weights_qkv, start, local_width, 1)
            gained = (rows * gain).astype(jnp.bfloat16)
            project = project + jnp.einsum(
                "cik,ckn->cin",
                jnp.broadcast_to(gained, (3,) + gained.shape),
                part,
                preferred_element_type=jnp.float32,
            )
        row_scale = lax.rsqrt(squares / model_width + NORM_EPSILON)[:, None]
        project = (project * row_scale).astype(jnp.bfloat16)
        project = project.reshape(3, length, local_heads, head_size)
        queries, key_heads, values = project[0], project[1], project[2]
        scores = (
            jnp.einsum("ihd,jhd->hij", queries, key_heads, preferred_element_type=jnp.float32)
            * score_scale
            + score_bias
        )
        row_max = jnp.max(scores, axis=2, keepdims=True)
        weights = jnp.exp(scores - row_max)
        attn_probs = (weights / jnp.sum(weights, axis=2, keepdims=True)).astype(jnp.bfloat16)
        head_mix = jnp.einsum(
            "hij,jhd->ihd", attn_probs, values, preferred_element_type=jnp.float32
        )
        head_mix = head_mix.astype(jnp.bfloat16).reshape(length, local_qkv)
        update = stream
        for peer, block in pieces(head_mix, "mp"):
            part = lax.dynamic_slice_in_dim(weights_out, peer * local_qkv, local_qkv, 0)
            update = update + jnp.dot(block, part, preferred_element_type=jnp.float32)
        return update.astype(jnp.bfloat16)

    def rotated(x, by):
        pairs = [(i, (i + by) % sections) for i in range(sections)]
        return lax.ppermute(x, "section", pairs)

    first = section_index == 0
    raw = micro_inputs[0]
    ticks = 2 * sections - 1
    current = raw
    result = raw
    for tick in range(ticks):
        if tick + 1 < sections:
            raw = rotated(raw, -1)
        out = attend(current)
        finished = tick - (sections - 1)
        if tick + 1 < ticks:
            sent = rotated(out, 1)
            current = jnp.where(first, raw, sent)
        if finished >= 0:
            owned = rotated(out, finished + 1) if tick + 1 < ticks and finished else (
                sent if tick + 1 < ticks else out)
            result = jnp.where(section_index == finished, owned, result)
    return result[None]


def solution(mesh):
    in_specs = (
        P(("dp", "section"), None, "mp"),
        P("section", None, None, "mp"),
        P("section", None, "mp"),
        P("section", None),
        P("mp", None),
    )
    out_specs = P(("dp", "section"), None, "mp")
    return jax.shard_map(shards, mesh=mesh, in_specs=in_specs, out_specs=out_specs, check_vma=False)
```

time: 188 us -> 116 us (0.62)
  blocking collectives: 93.7 us -> 0 us
  local copies, waits for them, and re-layouts: 35.9 us -> 1.34 us
  matrix products: 31.3 us -> 52.2 us
  waiting for transfers between devices: 7.42 us -> 26.7 us
  starting transfers between devices: 17.4 us -> 30.9 us
  other arithmetic: 1.03 us -> 3.66 us
    all_gather x6 -> x0, blocking collectives: 93.7 us -> none  [the longest x3 47.8 us: attend(): lax.all_gather(section_in, 'mp', axis=1, tiled=True).astype(jnp.float32)]
    dot_general x6 -> x24, matrix products: 29.7 us -> 49.8 us  [the longest x12 30.6 us: attend(): jnp.einsum('cik,ckn->cin', jnp.broadcast_to(gained, (3,) + gained.shape),...]
    ppermute x6 -> x21, waiting for transfers between devices: 7.42 us -> 26.7 us  [the longest x18 17.7 us: pieces(): other = lax.ppermute(x, axis, [(i, i ^ mask) for i in range(peers)])]
    while x8 -> x0, local copies, waits for them, and re-layouts: 17.3 us -> none  [the longest x2 16.8 us: shards(): final_pair = lax.fori_loop(0, ticks, conveyor_tick, (belt_start, blank))]
    unnamed x9 -> x4, local copies, waits for them, and re-layouts: 17 us -> 0.01 us
    ppermute x6 -> x21, starting transfers between devices: 17.4 us -> 30.9 us  [the longest x18 26.8 us: pieces(): other = lax.ppermute(x, axis, [(i, i ^ mask) for i in range(peers)])]
  transfers between devices with their start and end apart: 6 -> 21, of which waited for: 3 -> 10; matrix products, arithmetic and copies ran while one was open for 13% -> 37% of each run, Pallas kernels for 0% -> 0%
where the time goes in v1:
time: 116 us; the launch traced here: 115 us
  matrix products  52.2 us (45%)
  starting transfers between devices  30.9 us (27%)
  waiting for transfers between devices  26.7 us (23%)
  other arithmetic  3.66 us (3%)
  local copies, waits for them, and re-layouts  1.34 us (1%)
    dot_general x12, matrix products, attend(): jnp.einsum('cik,ckn->cin', jnp.broadcast_to(gained, (3,) + gained.shape),...  30.6 us
    ppermute x18, starting transfers between devices, pieces(): other = lax.ppermute(x, axis, [(i, i ^ mask) for i in range(peers)])  26.8 us
    dot_general x12, matrix products, attend(): update = update + jnp.dot(block, part, preferred_element_type=jnp.float32)  19.2 us
    ppermute x18, waiting for transfers between devices, pieces(): other = lax.ppermute(x, axis, [(i, i ^ mask) for i in range(peers)])  17.7 us
    ppermute x3, waiting for transfers between devices, rotated(): return lax.ppermute(x, 'section', pairs)  8.92 us
    ppermute x3, starting transfers between devices, rotated(): return lax.ppermute(x, 'section', pairs)  4.14 us
  transfers between devices with their start and end apart: 21, of which 10 were waited for; matrix products, arithmetic and copies ran while one was open for 37% of the time, Pallas kernels for 0%

profile of v1, /device:TPU:0, one launch (start us, length us, event | category | flops | bytes accessed | tf_op | source)
XLA Modules:
  0.0 115.3 jit_solution(3437802595431569075)
XLA Ops:
  0.0 3.0 %collective-permute-start = (bf16[64,1024]{1,0:T(8,128)(2,1)}, bf16[64,1024]{1,0:T(8,128)(2,1)S(1)}, u32[]{:S(2)}, u32[]{:S(2)}) collective-permute-start(bf16[64,1024]{1,0:T(8,128)(2,1)} %bitcast.145), channel_id=1, source_target_pairs={{0,4},{4,0},{1,5},{5,1},{2,6},{6,2},{3,7},{7,3},{8,12},{12,8},{9,1... | collective-permute-start | bytes 393224 | tf_op jit(solution)/shard_map/ppermute | solution.py:108
  3.0 2.6 %collective-permute-start.2 = (bf16[64,1024]{1,0:T(8,128)(2,1)}, bf16[64,1024]{1,0:T(8,128)(2,1)S(1)}, u32[]{:S(2)}, u32[]{:S(2)}) collective-permute-start(bf16[64,1024]{1,0:T(8,128)(2,1)} %bitcast.146), channel_id=1, source_target_pairs={{0,2},{1,3},{2,0},{3,1},{4,6},{5,7},{6,4},{7,5},{8,10},{9,11},{10,... | collective-permute-start | bytes 393224 | tf_op jit(solution)/shard_map/ppermute | solution.py:41
  10.6 2.6 %fusion.25 = f32[3,64,512]{2,1,0:T(8,128)S(1)} fusion(bf16[1,4096,3,512]{3,1,2,0:T(8,128)(2,1)} %param.7, s32[]{:T(128)S(6)} %select_n.76, bf16[64,1024]{1,0:T(8,128)(2,1)S(1)} %get-tuple-element.35), kind=kOutput, calls=%fused_computation.25 | convolution fusion | flops 201326592 | bytes 3670020 | tf_op jit(solution)/shard_map/cik,ckn->cin/dot_general | solution.py:78
  13.1 2.7 %collective-permute-done.2 = bf16[64,1024]{1,0:T(8,128)(2,1)S(1)} collective-permute-done((bf16[64,1024]{1,0:T(8,128)(2,1)}, bf16[64,1024]{1,0:T(8,128)(2,1)S(1)}, u32[]{:S(2)}, u32[]{:S(2)}) %collective-permute-start.2) | collective-permute-done | bytes 131104 | tf_op jit(solution)/shard_map/ppermute | solution.py:41
  15.9 2.5 %fusion.13 = f32[3,64,512]{2,1,0:T(8,128)S(1)} fusion(bf16[1,4096,3,512]{3,1,2,0:T(8,128)(2,1)} %param.7, s32[]{:T(128)S(6)} %select_n.78, bf16[64,1024]{1,0:T(8,128)(2,1)S(1)} %get-tuple-element.37), kind=kOutput, calls=%fused_computation.13 | convolution fusion | flops 201326592 | bytes 3670020 | tf_op jit(solution)/shard_map/cik,ckn->cin/dot_general | solution.py:78
  18.7 2.6 %fusion.75 = f32[3,64,512]{2,1,0:T(8,128)S(1)} fusion(f32[3,64,512]{2,1,0:T(8,128)S(1)} %fusion.13, f32[3,64,512]{2,1,0:T(8,128)S(1)} %fusion.25, bf16[1,4096,3,512]{3,1,2,0:T(8,128)(2,1)} %param.7, s32[]{:T(128)S(6)} %select_n.77, bf16[64,1024]{1,0:T(8,128)(2,1)S(1)} %get-tuple-element.33), kind=kOutput, calls=%fused_computation.53 | convolution fusion | flops 201523200 | bytes 4456452 | tf_op jit(solution)/shard_map/cik,ckn->cin/dot_general | solution.py:78
  21.4 2.6 %fusion.78 = bf16[3,64,512]{2,1,0:T(8,128)(2,1)S(1)} fusion(f32[3,64,512]{2,1,0:T(8,128)S(1)} %fusion.75, bf16[1,4096,3,512]{3,1,2,0:T(8,128)(2,1)} %param.7, s32[]{:T(128)S(6)} %select_n.79, f32[64]{0:T(128)S(1)} %add_rsqrt_fusion.2, bf16[64,1024]{1,0:T(8,128)(2,1)S(1)} %get-tuple-element.30), kind=kOutput, calls=%fused_computation.54 | convolution fusion | flops 201621504 | bytes 3866884 | tf_op jit(solution)/shard_map/cik,ckn->cin/dot_general | solution.py:78
  24.9 2.5 %collective-permute-start.6 = (bf16[64,512]{0,1:T(8,128)(2,1)S(1)}, bf16[64,512]{0,1:T(8,128)(2,1)S(1)}, u32[]{:S(2)}, u32[]{:S(2)}) collective-permute-start(bf16[64,512]{0,1:T(8,128)(2,1)S(1)} %bitcast.157), channel_id=1, source_target_pairs={{0,3},{1,2},{2,1},{3,0},{4,7},{5,6},{6,5},{7,4},{8,11},{9,10},{10,... | collective-permute-start | bytes 196616 | tf_op jit(solution)/shard_map/ppermute | solution.py:41
  39.6 4.5 %collective-permute-done.7 = bf16[64,1024]{1,0:T(8,128)(2,1)S(1)} collective-permute-done((bf16[64,1024]{1,0:T(8,128)(2,1)S(1)}, bf16[64,1024]{1,0:T(8,128)(2,1)S(1)}, u32[]{:S(2)}, u32[]{:S(2)}) %collective-permute-start.7) | collective-permute-done | bytes 131104 | tf_op jit(solution)/shard_map/ppermute | solution.py:108
  44.8 2.8 %collective-permute-start.8 = (bf16[64,1024]{1,0:T(8,128)(2,1)S(1)}, bf16[64,1024]{1,0:T(8,128)(2,1)S(1)}, u32[]{:S(2)}, u32[]{:S(2)}) collective-permute-start(bf16[64,1024]{1,0:T(8,128)(2,1)S(1)} %get-tuple-element.8), channel_id=1, source_target_pairs={{0,1},{1,0},{2,3},{3,2},{4,5},{5,4},{6,7},{7,6},{8,9},{9,8},{10,11... | collective-permute-start | bytes 393224 | tf_op jit(solution)/shard_map/ppermute | solution.py:41
  48.7 2.5 %fusion.23 = f32[3,64,512]{2,1,0:T(8,128)S(1)} fusion(bf16[1,4096,3,512]{3,1,2,0:T(8,128)(2,1)} %param.7, s32[]{:T(128)S(6)} %select_n.76, bf16[64,1024]{1,0:T(8,128)(2,1)S(1)} %fusion.160), kind=kOutput, calls=%fused_computation.23 | convolution fusion | flops 201326592 | bytes 3670020 | tf_op jit(solution)/shard_map/cik,ckn->cin/dot_general | solution.py:78
  51.3 4.3 %collective-permute-done.9 = bf16[64,1024]{1,0:T(8,128)(2,1)S(1)} collective-permute-done((bf16[64,1024]{1,0:T(8,128)(2,1)S(1)}, bf16[64,1024]{1,0:T(8,128)(2,1)S(1)}, u32[]{:S(2)}, u32[]{:S(2)}) %collective-permute-start.9) | collective-permute-done | bytes 131104 | tf_op jit(solution)/shard_map/ppermute | solution.py:41
  55.7 2.5 %fusion.11 = f32[3,64,512]{2,1,0:T(8,128)S(1)} fusion(bf16[1,4096,3,512]{3,1,2,0:T(8,128)(2,1)} %param.7, s32[]{:T(128)S(6)} %select_n.78, bf16[64,1024]{1,0:T(8,128)(2,1)S(1)} %get-tuple-element.29), kind=kOutput, calls=%fused_computation.11 | convolution fusion | flops 201326592 | bytes 3670020 | tf_op jit(solution)/shard_map/cik,ckn->cin/dot_general | solution.py:78
  58.4 2.6 %fusion.72 = f32[3,64,512]{2,1,0:T(8,128)S(1)} fusion(f32[3,64,512]{2,1,0:T(8,128)S(1)} %fusion.11, f32[3,64,512]{2,1,0:T(8,128)S(1)} %fusion.23, bf16[1,4096,3,512]{3,1,2,0:T(8,128)(2,1)} %param.7, s32[]{:T(128)S(6)} %select_n.77, bf16[64,1024]{1,0:T(8,128)(2,1)S(1)} %get-tuple-element.27), kind=kOutput, calls=%fused_computation.52 | convolution fusion | flops 201523200 | bytes 4456452 | tf_op jit(solution)/shard_map/cik,ckn->cin/dot_general | solution.py:78
  61.1 2.6 %fusion.81 = bf16[3,64,512]{2,1,0:T(8,128)(2,1)S(1)} fusion(f32[3,64,512]{2,1,0:T(8,128)S(1)} %fusion.72, bf16[1,4096,3,512]{3,1,2,0:T(8,128)(2,1)} %param.7, s32[]{:T(128)S(6)} %select_n.79, f32[64]{0:T(128)S(1)} %add_rsqrt_fusion.1, bf16[64,1024]{1,0:T(8,128)(2,1)S(1)} %get-tuple-element.24), kind=kOutput, calls=%fused_computation.55 | convolution fusion | flops 201621504 | bytes 3866884 | tf_op jit(solution)/shard_map/cik,ckn->cin/dot_general | solution.py:78
  66.2 2.9 %collective-permute-start.11 = (bf16[64,512]{0,1:T(8,128)(2,1)S(1)}, bf16[64,512]{0,1:T(8,128)(2,1)S(1)}, u32[]{:S(2)}, u32[]{:S(2)}) collective-permute-start(bf16[64,512]{0,1:T(8,128)(2,1)S(1)} %bitcast.155), channel_id=1, source_target_pairs={{0,1},{1,0},{2,3},{3,2},{4,5},{5,4},{6,7},{7,6},{8,9},{9,8},{10,11... | collective-permute-start | bytes 196616 | tf_op jit(solution)/shard_map/ppermute | solution.py:41
  69.1 2.6 %collective-permute-done.13 = bf16[64,512]{0,1:T(8,128)(2,1)S(1)} collective-permute-done((bf16[64,512]{0,1:T(8,128)(2,1)S(1)}, bf16[64,512]{0,1:T(8,128)(2,1)S(1)}, u32[]{:S(2)}, u32[]{:S(2)}) %collective-permute-start.13) | collective-permute-done | bytes 65568 | tf_op jit(solution)/shard_map/ppermute | solution.py:41
  79.5 4.5 %collective-permute-done.14 = bf16[64,1024]{1,0:T(8,128)(2,1)S(1)} collective-permute-done((bf16[64,1024]{1,0:T(8,128)(2,1)S(1)}, bf16[64,1024]{1,0:T(8,128)(2,1)S(1)}, u32[]{:S(2)}, u32[]{:S(2)}) %collective-permute-start.14) | collective-permute-done | bytes 131104 | tf_op jit(solution)/shard_map/ppermute | solution.py:108
  88.7 2.5 %fusion.21 = f32[3,64,512]{2,1,0:T(8,128)S(1)} fusion(bf16[1,4096,3,512]{3,1,2,0:T(8,128)(2,1)} %param.7, s32[]{:T(128)S(6)} %select_n.76, bf16[64,1024]{1,0:T(8,128)(2,1)S(1)} %fusion.162), kind=kOutput, calls=%fused_computation.21 | convolution fusion | flops 201326592 | bytes 3670020 | tf_op jit(solution)/shard_map/cik,ckn->cin/dot_general | solution.py:78
  91.4 2.5 %fusion.9 = f32[3,64,512]{2,1,0:T(8,128)S(1)} fusion(bf16[1,4096,3,512]{3,1,2,0:T(8,128)(2,1)} %param.7, s32[]{:T(128)S(6)} %select_n.78, bf16[64,1024]{1,0:T(8,128)(2,1)S(1)} %get-tuple-element.23), kind=kOutput, calls=%fused_computation.9 | convolution fusion | flops 201326592 | bytes 3670020 | tf_op jit(solution)/shard_map/cik,ckn->cin/dot_general | solution.py:78
  94.1 2.6 %fusion.69 = f32[3,64,512]{2,1,0:T(8,128)S(1)} fusion(f32[3,64,512]{2,1,0:T(8,128)S(1)} %fusion.9, f32[3,64,512]{2,1,0:T(8,128)S(1)} %fusion.21, bf16[1,4096,3,512]{3,1,2,0:T(8,128)(2,1)} %param.7, s32[]{:T(128)S(6)} %select_n.77, bf16[64,1024]{1,0:T(8,128)(2,1)S(1)} %get-tuple-element.21), kind=kOutput, calls=%fused_computation.51 | convolution fusion | flops 201523200 | bytes 4456452 | tf_op jit(solution)/shard_map/cik,ckn->cin/dot_general | solution.py:78
  96.8 2.6 %fusion.84 = bf16[3,64,512]{2,1,0:T(8,128)(2,1)S(1)} fusion(f32[3,64,512]{2,1,0:T(8,128)S(1)} %fusion.69, bf16[1,4096,3,512]{3,1,2,0:T(8,128)(2,1)} %param.7, s32[]{:T(128)S(6)} %select_n.79, f32[64]{0:T(128)S(1)} %add_rsqrt_fusion, bf16[64,1024]{1,0:T(8,128)(2,1)S(1)} %get-tuple-element.18), kind=kOutput, calls=%fused_computation.56 | convolution fusion | flops 201621504 | bytes 3866884 | tf_op jit(solution)/shard_map/cik,ckn->cin/dot_general | solution.py:78
  101.9 2.9 %collective-permute-start.18 = (bf16[64,512]{0,1:T(8,128)(2,1)S(1)}, bf16[64,512]{0,1:T(8,128)(2,1)S(1)}, u32[]{:S(2)}, u32[]{:S(2)}) collective-permute-start(bf16[64,512]{0,1:T(8,128)(2,1)S(1)} %bitcast.151), channel_id=1, source_target_pairs={{0,1},{1,0},{2,3},{3,2},{4,5},{5,4},{6,7},{7,6},{8,9},{9,8},{10,11... | collective-permute-start | bytes 196616 | tf_op jit(solution)/shard_map/ppermute | solution.py:41
  104.7 2.6 %collective-permute-done.20 = bf16[64,512]{0,1:T(8,128)(2,1)S(1)} collective-permute-done((bf16[64,512]{0,1:T(8,128)(2,1)S(1)}, bf16[64,512]{0,1:T(8,128)(2,1)S(1)}, u32[]{:S(2)}, u32[]{:S(2)}) %collective-permute-start.20) | collective-permute-done | bytes 65568 | tf_op jit(solution)/shard_map/ppermute | solution.py:41
  (88 shorter events, 46.5 us)
Async XLA Ops:
  0.0 9.2 %copy-start = (f32[8,32]{1,0:T(8,128)S(1)}, f32[8,32]{1,0:T(8,128)}, u32[]{:S(2)}) copy-start(f32[8,32]{1,0:T(8,128)} %param.10) | copy-start | bytes 3076
  0.0 39.6 %collective-permute-start = (bf16[64,1024]{1,0:T(8,128)(2,1)}, bf16[64,1024]{1,0:T(8,128)(2,1)S(1)}, u32[]{:S(2)}, u32[]{:S(2)}) collective-permute-start(bf16[64,1024]{1,0:T(8,128)(2,1)} %bitcast.145), channel_id=1, source_target_pairs={{0,4},{4,0},{1,5},{5,1},{2,6},{6,2},{3,7},{7,3},{8,12},{12,8},{9,1... | collective-permute-start | bytes 393224 | tf_op jit(solution)/shard_map/ppermute | solution.py:108
  3.0 12.8 %collective-permute-start.2 = (bf16[64,1024]{1,0:T(8,128)(2,1)}, bf16[64,1024]{1,0:T(8,128)(2,1)S(1)}, u32[]{:S(2)}, u32[]{:S(2)}) collective-permute-start(bf16[64,1024]{1,0:T(8,128)(2,1)} %bitcast.146), channel_id=1, source_target_pairs={{0,2},{1,3},{2,0},{3,1},{4,6},{5,7},{6,4},{7,5},{8,10},{9,11},{10,... | collective-permute-start | bytes 393224 | tf_op jit(solution)/shard_map/ppermute | solution.py:41
  5.6 12.9 %collective-permute-start.1 = (bf16[64,1024]{1,0:T(8,128)(2,1)}, bf16[64,1024]{1,0:T(8,128)(2,1)S(1)}, u32[]{:S(2)}, u32[]{:S(2)}) collective-permute-start(bf16[64,1024]{1,0:T(8,128)(2,1)} %bitcast.147), channel_id=1, source_target_pairs={{0,1},{1,0},{2,3},{3,2},{4,5},{5,4},{6,7},{7,6},{8,9},{9,8},{10,11... | collective-permute-start | bytes 393224 | tf_op jit(solution)/shard_map/ppermute | solution.py:41
  7.2 14.1 %collective-permute-start.3 = (bf16[64,1024]{1,0:T(8,128)(2,1)}, bf16[64,1024]{1,0:T(8,128)(2,1)S(1)}, u32[]{:S(2)}, u32[]{:S(2)}) collective-permute-start(bf16[64,1024]{1,0:T(8,128)(2,1)} %bitcast.148), channel_id=1, source_target_pairs={{0,3},{1,2},{2,1},{3,0},{4,7},{5,6},{6,5},{7,4},{8,11},{9,10},{10,... | collective-permute-start | bytes 393224 | tf_op jit(solution)/shard_map/ppermute | solution.py:41
  21.2 8.1 %copy-start.1 = (bf16[1,64,1024]{2,1,0:T(8,128)(2,1)S(1)}, bf16[1,64,1024]{2,1,0:T(8,128)(2,1)}, u32[]{:S(2)}) copy-start(bf16[1,64,1024]{2,1,0:T(8,128)(2,1)} %param.6) | copy-start | bytes 393220
  24.9 8.3 %collective-permute-start.6 = (bf16[64,512]{0,1:T(8,128)(2,1)S(1)}, bf16[64,512]{0,1:T(8,128)(2,1)S(1)}, u32[]{:S(2)}, u32[]{:S(2)}) collective-permute-start(bf16[64,512]{0,1:T(8,128)(2,1)S(1)} %bitcast.157), channel_id=1, source_target_pairs={{0,3},{1,2},{2,1},{3,0},{4,7},{5,6},{6,5},{7,4},{8,11},{9,10},{10,... | collective-permute-start | bytes 196616 | tf_op jit(solution)/shard_map/ppermute | solution.py:41
  27.4 8.5 %collective-permute-start.5 = (bf16[64,512]{0,1:T(8,128)(2,1)S(1)}, bf16[64,512]{0,1:T(8,128)(2,1)S(1)}, u32[]{:S(2)}, u32[]{:S(2)}) collective-permute-start(bf16[64,512]{0,1:T(8,128)(2,1)S(1)} %bitcast.158), channel_id=1, source_target_pairs={{0,2},{1,3},{2,0},{3,1},{4,6},{5,7},{6,4},{7,5},{8,10},{9,11},{10,... | collective-permute-start | bytes 196616 | tf_op jit(solution)/shard_map/ppermute | solution.py:41
  27.4 10.0 %collective-permute-start.4 = (bf16[64,512]{0,1:T(8,128)(2,1)S(1)}, bf16[64,512]{0,1:T(8,128)(2,1)S(1)}, u32[]{:S(2)}, u32[]{:S(2)}) collective-permute-start(bf16[64,512]{0,1:T(8,128)(2,1)S(1)} %bitcast.159), channel_id=1, source_target_pairs={{0,1},{1,0},{2,3},{3,2},{4,5},{5,4},{6,7},{7,6},{8,9},{9,8},{10,11... | collective-permute-start | bytes 196616 | tf_op jit(solution)/shard_map/ppermute | solution.py:41
  39.0 5.0 %collective-permute-start.7 = (bf16[64,1024]{1,0:T(8,128)(2,1)S(1)}, bf16[64,1024]{1,0:T(8,128)(2,1)S(1)}, u32[]{:S(2)}, u32[]{:S(2)}) collective-permute-start(bf16[64,1024]{1,0:T(8,128)(2,1)S(1)} %fusion.103), channel_id=1, source_target_pairs={{0,4},{4,0},{1,5},{5,1},{2,6},{6,2},{3,7},{7,3},{8,12},{12,8},{9,1... | collective-permute-start | bytes 393224 | tf_op jit(solution)/shard_map/ppermute | solution.py:108
  44.2 11.4 %collective-permute-start.9 = (bf16[64,1024]{1,0:T(8,128)(2,1)S(1)}, bf16[64,1024]{1,0:T(8,128)(2,1)S(1)}, u32[]{:S(2)}, u32[]{:S(2)}) collective-permute-start(bf16[64,1024]{1,0:T(8,128)(2,1)S(1)} %get-tuple-element.8), channel_id=1, source_target_pairs={{0,2},{1,3},{2,0},{3,1},{4,6},{5,7},{6,4},{7,5},{8,10},{9,11},{10,... | collective-permute-start | bytes 393224 | tf_op jit(solution)/shard_map/ppermute | solution.py:41
  44.8 13.5 %collective-permute-start.8 = (bf16[64,1024]{1,0:T(8,128)(2,1)S(1)}, bf16[64,1024]{1,0:T(8,128)(2,1)S(1)}, u32[]{:S(2)}, u32[]{:S(2)}) collective-permute-start(bf16[64,1024]{1,0:T(8,128)(2,1)S(1)} %get-tuple-element.8), channel_id=1, source_target_pairs={{0,1},{1,0},{2,3},{3,2},{4,5},{5,4},{6,7},{7,6},{8,9},{9,8},{10,11... | collective-permute-start | bytes 393224 | tf_op jit(solution)/shard_map/ppermute | solution.py:41
  47.5 13.4 %collective-permute-start.10 = (bf16[64,1024]{1,0:T(8,128)(2,1)S(1)}, bf16[64,1024]{1,0:T(8,128)(2,1)S(1)}, u32[]{:S(2)}, u32[]{:S(2)}) collective-permute-start(bf16[64,1024]{1,0:T(8,128)(2,1)S(1)} %get-tuple-element.8), channel_id=1, source_target_pairs={{0,3},{1,2},{2,1},{3,0},{4,7},{5,6},{6,5},{7,4},{8,11},{9,10},{10,... | collective-permute-start | bytes 393224 | tf_op jit(solution)/shard_map/ppermute | solution.py:41
  64.6 7.0 %collective-permute-start.13 = (bf16[64,512]{0,1:T(8,128)(2,1)S(1)}, bf16[64,512]{0,1:T(8,128)(2,1)S(1)}, u32[]{:S(2)}, u32[]{:S(2)}) collective-permute-start(bf16[64,512]{0,1:T(8,128)(2,1)S(1)} %bitcast.153), channel_id=1, source_target_pairs={{0,3},{1,2},{2,1},{3,0},{4,7},{5,6},{6,5},{7,4},{8,11},{9,10},{10,... | collective-permute-start | bytes 196616 | tf_op jit(solution)/shard_map/ppermute | solution.py:41
  66.2 8.1 %collective-permute-start.12 = (bf16[64,512]{0,1:T(8,128)(2,1)S(1)}, bf16[64,512]{0,1:T(8,128)(2,1)S(1)}, u32[]{:S(2)}, u32[]{:S(2)}) collective-permute-start(bf16[64,512]{0,1:T(8,128)(2,1)S(1)} %bitcast.154), channel_id=1, source_target_pairs={{0,2},{1,3},{2,0},{3,1},{4,6},{5,7},{6,4},{7,5},{8,10},{9,11},{10,... | collective-permute-start | bytes 196616 | tf_op jit(solution)/shard_map/ppermute | solution.py:41
  66.2 9.6 %collective-permute-start.11 = (bf16[64,512]{0,1:T(8,128)(2,1)S(1)}, bf16[64,512]{0,1:T(8,128)(2,1)S(1)}, u32[]{:S(2)}, u32[]{:S(2)}) collective-permute-start(bf16[64,512]{0,1:T(8,128)(2,1)S(1)} %bitcast.155), channel_id=1, source_target_pairs={{0,1},{1,0},{2,3},{3,2},{4,5},{5,4},{6,7},{7,6},{8,9},{9,8},{10,11... | collective-permute-start | bytes 196616 | tf_op jit(solution)/shard_map/ppermute | solution.py:41
  79.0 5.0 %collective-permute-start.14 = (bf16[64,1024]{1,0:T(8,128)(2,1)S(1)}, bf16[64,1024]{1,0:T(8,128)(2,1)S(1)}, u32[]{:S(2)}, u32[]{:S(2)}) collective-permute-start(bf16[64,1024]{1,0:T(8,128)(2,1)S(1)} %fusion.101), channel_id=1, source_target_pairs={{0,4},{4,0},{1,5},{5,1},{2,6},{6,2},{3,7},{7,3},{8,12},{12,8},{9,1... | collective-permute-start | bytes 393224 | tf_op jit(solution)/shard_map/ppermute | solution.py:108
  84.1 7.1 %collective-permute-start.16 = (bf16[64,1024]{1,0:T(8,128)(2,1)S(1)}, bf16[64,1024]{1,0:T(8,128)(2,1)S(1)}, u32[]{:S(2)}, u32[]{:S(2)}) collective-permute-start(bf16[64,1024]{1,0:T(8,128)(2,1)S(1)} %get-tuple-element.6), channel_id=1, source_target_pairs={{0,2},{1,3},{2,0},{3,1},{4,6},{5,7},{6,4},{7,5},{8,10},{9,11},{10,... | collective-permute-start | bytes 393224 | tf_op jit(solution)/shard_map/ppermute | solution.py:41
  84.2 9.7 %collective-permute-start.15 = (bf16[64,1024]{1,0:T(8,128)(2,1)S(1)}, bf16[64,1024]{1,0:T(8,128)(2,1)S(1)}, u32[]{:S(2)}, u32[]{:S(2)}) collective-permute-start(bf16[64,1024]{1,0:T(8,128)(2,1)S(1)} %get-tuple-element.6), channel_id=1, source_target_pairs={{0,1},{1,0},{2,3},{3,2},{4,5},{5,4},{6,7},{7,6},{8,9},{9,8},{10,11... | collective-permute-start | bytes 393224 | tf_op jit(solution)/shard_map/ppermute | solution.py:41
  86.4 10.3 %collective-permute-start.17 = (bf16[64,1024]{1,0:T(8,128)(2,1)S(1)}, bf16[64,1024]{1,0:T(8,128)(2,1)S(1)}, u32[]{:S(2)}, u32[]{:S(2)}) collective-permute-start(bf16[64,1024]{1,0:T(8,128)(2,1)S(1)} %get-tuple-element.6), channel_id=1, source_target_pairs={{0,3},{1,2},{2,1},{3,0},{4,7},{5,6},{6,5},{7,4},{8,11},{9,10},{10,... | collective-permute-start | bytes 393224 | tf_op jit(solution)/shard_map/ppermute | solution.py:41
  100.3 7.0 %collective-permute-start.20 = (bf16[64,512]{0,1:T(8,128)(2,1)S(1)}, bf16[64,512]{0,1:T(8,128)(2,1)S(1)}, u32[]{:S(2)}, u32[]{:S(2)}) collective-permute-start(bf16[64,512]{0,1:T(8,128)(2,1)S(1)} %bitcast.149), channel_id=1, source_target_pairs={{0,3},{1,2},{2,1},{3,0},{4,7},{5,6},{6,5},{7,4},{8,11},{9,10},{10,... | collective-permute-start | bytes 196616 | tf_op jit(solution)/shard_map/ppermute | solution.py:41
  101.9 8.1 %collective-permute-start.19 = (bf16[64,512]{0,1:T(8,128)(2,1)S(1)}, bf16[64,512]{0,1:T(8,128)(2,1)S(1)}, u32[]{:S(2)}, u32[]{:S(2)}) collective-permute-start(bf16[64,512]{0,1:T(8,128)(2,1)S(1)} %bitcast.150), channel_id=1, source_target_pairs={{0,2},{1,3},{2,0},{3,1},{4,6},{5,7},{6,4},{7,5},{8,10},{9,11},{10,... | collective-permute-start | bytes 196616 | tf_op jit(solution)/shard_map/ppermute | solution.py:41
  101.9 9.6 %collective-permute-start.18 = (bf16[64,512]{0,1:T(8,128)(2,1)S(1)}, bf16[64,512]{0,1:T(8,128)(2,1)S(1)}, u32[]{:S(2)}, u32[]{:S(2)}) collective-permute-start(bf16[64,512]{0,1:T(8,128)(2,1)S(1)} %bitcast.151), channel_id=1, source_target_pairs={{0,1},{1,0},{2,3},{3,2},{4,5},{5,4},{6,7},{7,6},{8,9},{9,8},{10,11... | collective-permute-start | bytes 196616 | tf_op jit(solution)/shard_map/ppermute | solution.py:41

commit v2 on v1

v2 whole, which is shorter than its diff:
```python
import math

import jax
import jax.numpy as jnp
import numpy as np
from jax import lax
from jax.experimental import pallas as pl
from jax.experimental.pallas import tpu as pltpu
from jax.sharding import PartitionSpec as P

REACH = 128
NORM_EPSILON = 0.1
MOST_DIRECT = 4
LANES = 128
F32 = jnp.float32
BF16 = jnp.bfloat16
VMEM = pltpu.VMEM


def bucket_table(length, bucket_count, reach_limit):
    offset = np.arange(length)[None, :] - np.arange(length)[:, None]
    half_count = bucket_count // 2
    upper_side = (offset > 0).astype(np.int32) * half_count
    distance = np.abs(offset)
    exact_count = half_count // 2
    scaled = (
        np.log(np.maximum(distance, 1) / exact_count)
        / np.log(reach_limit / exact_count)
        * (half_count - exact_count)
    )
    far_bucket = np.minimum(exact_count + scaled.astype(np.int32), half_count - 1)
    return (upper_side + np.where(distance < exact_count, distance, far_bucket)).astype(np.int32)


def swap_masks(peers):
    if peers & (peers - 1) or peers > MOST_DIRECT:
        return None
    return sorted(range(1, peers), key=lambda mask: (bin(mask).count("1"), mask))


def from_peers(x, axis):
    peers = lax.axis_size(axis)
    masks = swap_masks(peers)
    if masks is None:
        return [lax.all_gather(x, axis, axis=0, tiled=False)]
    return [lax.ppermute(x, axis, [(i, i ^ mask) for i in range(peers)]) for mask in masks]


def peer_blocks(refs, axis):
    peers = lax.axis_size(axis)
    me = lax.axis_index(axis)
    masks = swap_masks(peers)
    if masks is None:
        turned = [lax.rem(me + step, peers) for step in range(1, peers)]
        return [(peer, refs[0][peer]) for peer in turned]
    return [(me ^ mask, ref[...]) for mask, ref in zip(masks, refs)]


def rows_of(peer, count):
    return pl.ds(pl.multiple_of(peer * count, count), count)


def call(body, outs, *args, specs=None, scratch=(), limit=8):
    specs = specs or [pl.BlockSpec(memory_space=VMEM)] * len(args)
    return pl.pallas_call(
        body,
        in_specs=specs,
        out_specs=tuple(pl.BlockSpec(memory_space=VMEM) for _ in outs),
        out_shape=tuple(outs),
        scratch_shapes=list(scratch),
        compiler_params=pltpu.CompilerParams(vmem_limit_bytes=limit << 20),
    )(*args)


def add_part(peer, block, gain_ref, weight_ref, total_ref, squares):
    width = block.shape[1]
    rows = block.astype(F32)
    gain = gain_ref[:, rows_of(peer, width)].astype(F32)
    gained = (rows * gain).astype(BF16)
    for lane in range(0, width, LANES):
        tile = rows[:, lane : lane + LANES]
        squares = squares + tile * tile
    for kind in range(weight_ref.shape[0]):
        part = weight_ref[kind, rows_of(peer, width), :]
        total_ref[kind] += jnp.dot(gained, part, preferred_element_type=F32)
    return squares


def own_part(peer, block, gain_ref, weight_ref, total_ref, squares_ref):
    total_ref[...] = jnp.zeros_like(total_ref)
    squares = jnp.zeros(squares_ref.shape, F32)
    squares_ref[...] = add_part(peer, block, gain_ref, weight_ref, total_ref, squares)


def load_kernel(x_ref, gain_ref, qkv_ref, out_ref, table_ref, grid_ref,
                held_qkv, held_out, total_ref, squares_ref, bias_ref, sems):
    peers = lax.axis_size("mp")
    me = lax.axis_index("mp")
    width = x_ref.shape[1]
    copies = []
    for step in range(peers):
        rows = rows_of(lax.rem(me + step, peers), width)
        copies.append(pltpu.make_async_copy(
            qkv_ref.at[:, rows, :], held_qkv.at[:, rows, :], sems.at[step]))
    copies.append(pltpu.make_async_copy(out_ref, held_out, sems.at[peers]))
    for copy in copies:
        copy.start()
    heads, buckets = table_ref.shape
    length = grid_ref.shape[0]

    def one_head(head, carry):
        grid = grid_ref[...]
        bias = jnp.zeros(grid.shape, F32)
        for bucket in range(buckets):
            bias = jnp.where(grid == bucket, table_ref[head, bucket], bias)
        bias_ref[rows_of(head, length), :] = bias
        return carry

    lax.fori_loop(0, heads, one_head, 0)
    copies[0].wait()
    own_part(me, x_ref[...], gain_ref, held_qkv, total_ref, squares_ref)
    for copy in copies[1:]:
        copy.wait()


def own_kernel(x_ref, gain_ref, held_qkv, total_ref, squares_ref):
    own_part(lax.axis_index("mp"), x_ref[...], gain_ref, held_qkv, total_ref, squares_ref)


def attend_kernel(head_size, model_width, *refs):
    *peer_refs, gain_ref, held_qkv, partial_ref, partial_squares, bias_ref, mix_ref, total_ref = refs
    total_ref[...] = partial_ref[...]
    squares = partial_squares[...]
    for peer, block in peer_blocks(peer_refs, "mp"):
        squares = add_part(peer, block, gain_ref, held_qkv, total_ref, squares)
    mean_square = jnp.sum(squares, axis=1, keepdims=True) / model_width
    row_scale = lax.rsqrt(mean_square + NORM_EPSILON)
    length, local_qkv = mix_ref.shape
    score_scale = 1.0 / math.sqrt(head_size)
    block_heads = LANES // head_size
    lane = lax.broadcasted_iota(jnp.int32, (length, LANES), 1) // head_size
    for block in range(local_qkv // LANES):
        lanes = pl.ds(block * LANES, LANES)
        queries, keys, values = (total_ref[kind, :, lanes] * row_scale for kind in range(3))
        keys = keys.astype(BF16)
        values = values.astype(BF16)
        stacked = jnp.concatenate(
            [jnp.where(lane == head, queries, 0.0) for head in range(block_heads)], axis=0
        ).astype(BF16)
        scores = lax.dot_general(
            stacked, keys, (((1,), (1,)), ((), ())), preferred_element_type=F32)
        rows = pl.ds(block * block_heads * length, block_heads * length)
        scores = scores * score_scale + bias_ref[rows, :]
        weights = jnp.exp(scores - jnp.max(scores, axis=1, keepdims=True))
        probs = (weights / jnp.sum(weights, axis=1, keepdims=True)).astype(BF16)
        mixed = jnp.dot(probs, values, preferred_element_type=F32)
        mix = mixed[:length]
        for head in range(1, block_heads):
            mix = jnp.where(lane == head, mixed[head * length : (head + 1) * length], mix)
        mix_ref[:, lanes] = mix.astype(BF16)


def out_kernel(keep_section, *refs):
    *peer_refs, own_ref, held_out, stream_ref, kept_ref, result_ref = refs
    local_qkv = own_ref.shape[1]
    total = stream_ref[...].astype(F32)
    blocks = [(lax.axis_index("mp"), own_ref[...])] + peer_blocks(peer_refs, "mp")
    for peer, block in blocks:
        part = held_out[rows_of(peer, local_qkv), :]
        total += jnp.dot(block, part, preferred_element_type=F32)
    result = total.astype(BF16)
    if keep_section is not None:
        result = jnp.where(lax.axis_index("section") == keep_section, kept_ref[...], result)
    result_ref[...] = result


def pick_kernel(section, a_ref, b_ref, o_ref):
    o_ref[...] = jnp.where(lax.axis_index("section") == section, a_ref[...], b_ref[...])


def pick(section, a, b):
    return call(lambda *refs: pick_kernel(section, *refs), [VMEM(a.shape, a.dtype)], a, b)[0]


def shards(micro_inputs, qkv_weight, out_weight, norm_gain, position_bias):
    sections = lax.axis_size("section")
    peers = lax.axis_size("mp")
    length = micro_inputs.shape[1]
    model_width = qkv_weight.shape[1]
    local_heads, bucket_count = position_bias.shape
    local_qkv = qkv_weight.shape[3]
    head_size = local_qkv // local_heads
    weights_qkv = jnp.transpose(qkv_weight[0], (1, 0, 2))
    weights_out = out_weight[0]
    bucket_grid = jnp.asarray(bucket_table(length, bucket_count, REACH))

    total = VMEM((3, length, local_qkv), F32)
    squares = VMEM((length, LANES), F32)
    held = {}

    def attend(section_in, keep_section, kept):
        others = from_peers(section_in, "mp")
        if not held:
            vm = pl.BlockSpec(memory_space=VMEM)
            hbm = pl.BlockSpec(memory_space=pltpu.HBM)
            sm = pl.BlockSpec(memory_space=pltpu.SMEM)
            bias = VMEM((local_heads * length, length), F32)
            held["qkv"], held["out"], part, part_squares, held["bias"] = call(
                load_kernel,
                [VMEM(weights_qkv.shape, BF16), VMEM(weights_out.shape, BF16), total, squares, bias],
                section_in, norm_gain, weights_qkv, weights_out, position_bias, bucket_grid,
                specs=[vm, vm, hbm, hbm, sm, vm],
                scratch=[pltpu.SemaphoreType.DMA((peers + 1,))],
            )
        else:
            part, part_squares = call(
                own_kernel, [total, squares], section_in, norm_gain, held["qkv"])
        mix = call(
            lambda *refs: attend_kernel(head_size, model_width, *refs),
            [VMEM((length, local_qkv), BF16)],
            *others, norm_gain, held["qkv"], part, part_squares, held["bias"],
            scratch=[total],
        )[0]
        mixes = from_peers(mix, "mp")
        return call(
            lambda *refs: out_kernel(keep_section, *refs),
            [VMEM(section_in.shape, BF16)],
            *mixes, mix, held["out"], section_in, kept,
        )[0]

    def rotated(x, by):
        return lax.ppermute(x, "section", [(i, (i + by) % sections) for i in range(sections)])

    raw = micro_inputs[0]
    if sections == 2:
        handed = rotated(attend(raw, 1, raw), 1)
        finished = rotated(attend(handed, None, raw), 1)
        return attend(finished, 0, finished)[None]
    ticks = 2 * sections - 1
    current = raw
    result = raw
    for tick in range(ticks):
        if tick + 1 < sections:
            raw = rotated(raw, -1)
        out = attend(current, None, current)
        done = tick - (sections - 1)
        if tick + 1 < ticks:
            sent = rotated(out, 1)
            current = pick(0, raw, sent)
        if done >= 0:
            owned = rotated(out, done + 1) if done + 1 < sections else out
            result = pick(done, owned, result)
    return result[None]


def solution(mesh):
    in_specs = (
        P(("dp", "section"), None, "mp"),
        P("section", None, None, "mp"),
        P("section", None, "mp"),
        P("section", None),
        P("mp", None),
    )
    out_specs = P(("dp", "section"), None, "mp")
    return jax.shard_map(shards, mesh=mesh, in_specs=in_specs, out_specs=out_specs, check_vma=False)
```

time: 116 us -> 85 us (0.73)
  matrix products: 52.2 us -> 0 us
  Pallas kernels: 0 us -> 13.7 us
  local copies, waits for them, and re-layouts: 1.34 us -> 10.5 us
  other arithmetic: 3.66 us -> 0 us
  waiting for transfers between devices: 26.7 us -> 29.4 us
    dot_general x31 -> x0, matrix products: 52.2 us -> none  [the longest x12 30.6 us: attend(): jnp.einsum('cik,ckn->cin', jnp.broadcast_to(gained, (3,) + gained.shape),...]
    pallas_call x0 -> x9, Pallas kernels: none -> 13.7 us  [call(): pl.pallas_call(body, in_specs=specs, out_specs=tuple((pl.BlockSpec(memory...]
    unnamed x4 -> x15, local copies, waits for them, and re-layouts: 0.01 us -> 10.5 us
    ppermute x21 -> x20, waiting for transfers between devices: 26.7 us -> 29.4 us  [the longest x18 22.5 us: from_peers(): lax.ppermute(x, axis, [(i, i ^ mask) for i in range(peers)])]
    reduce_sum x9 -> x0, other arithmetic: 2.18 us -> none  [attend(): squares = squares + jnp.sum(rows * rows, axis=1)]
    convert_element_type x6 -> x0, other arithmetic: 1.21 us -> none  [the longest x1 0.73 us: shards(): gain_row = norm_gain[0].astype(jnp.float32)]
    ppermute x21 -> x20, starting transfers between devices: 30.9 us -> 30.9 us  [the longest x18 27.8 us: from_peers(): lax.ppermute(x, axis, [(i, i ^ mask) for i in range(peers)])]
  transfers between devices with their start and end apart: 21 -> 20, of which waited for: 10 -> 13; matrix products, arithmetic and copies ran while one was open for 37% -> 0% of each run, Pallas kernels for 0% -> 6%
where the time goes in v2:
time: 85 us; the launch traced here: 84.6 us
  starting transfers between devices  30.9 us (36%)
  waiting for transfers between devices  29.4 us (35%)
  Pallas kernels  13.7 us (16%)
  local copies, waits for them, and re-layouts  10.5 us (12%)
    ppermute x18, starting transfers between devices, from_peers(): lax.ppermute(x, axis, [(i, i ^ mask) for i in range(peers)])  27.8 us
    ppermute x18, waiting for transfers between devices, from_peers(): lax.ppermute(x, axis, [(i, i ^ mask) for i in range(peers)])  22.5 us
    pallas_call x9, Pallas kernels, call(): pl.pallas_call(body, in_specs=specs, out_specs=tuple((pl.BlockSpec(memory...  13.7 us
    unnamed x15, local copies, waits for them, and re-layouts  10.5 us
    ppermute x2, waiting for transfers between devices, rotated(): lax.ppermute(x, 'section', [(i, (i + by) % sections) for i in range(secti...  6.9 us
    ppermute x2, starting transfers between devices, rotated(): lax.ppermute(x, 'section', [(i, (i + by) % sections) for i in range(secti...  3.17 us
  transfers between devices with their start and end apart: 20, of which 13 were waited for; matrix products, arithmetic and copies ran while one was open for 0% of the time, Pallas kernels for 6%

profile of v2, /device:TPU:0, one launch (start us, length us, event | category | flops | bytes accessed | tf_op | source)
XLA Modules:
  0.0 84.6 jit_solution(17551473348964316755)
XLA Ops:
  0.0 5.1 %collective-permute-start.2 = (bf16[64,1024]{1,0:T(8,128)(2,1)}, bf16[64,1024]{1,0:T(8,128)(2,1)S(1)}, u32[]{:S(2)}, u32[]{:S(2)}) collective-permute-start(bf16[64,1024]{1,0:T(8,128)(2,1)} %bitcast.9), channel_id=1, source_target_pairs={{0,3},{1,2},{2,1},{3,0},{4,7},{5,6},{6,5},{7,4},{8,11},{9,10},{10,... | collective-permute-start | bytes 393224 | tf_op jit(solution)/shard_map/ppermute | solution.py:46
  5.6 4.6 %copy-done = bf16[1,4096,3,512]{3,1,2,0:T(8,128)(2,1)S(1)} copy-done((bf16[1,4096,3,512]{3,1,2,0:T(8,128)(2,1)S(1)}, bf16[1,4096,3,512]{3,1,2,0:T(8,128)(2,1)}, u32[]{:S(2)}) %copy-start) | copy-done | bytes 12582936
  10.2 2.2 %copy-done.1 = bf16[1,2048,1024]{2,1,0:T(8,128)(2,1)S(1)} copy-done((bf16[1,2048,1024]{2,1,0:T(8,128)(2,1)S(1)}, bf16[1,2048,1024]{2,1,0:T(8,128)(2,1)}, u32[]{:S(2)}) %copy-start.1) | copy-done | bytes 4194328
  15.5 3.4 %shard_map.64 = (bf16[3,4096,512]{2,1,0:T(8,128)(2,1)S(1)}, bf16[2048,1024]{1,0:T(8,128)(2,1)S(1)}, f32[3,64,512]{2,1,0:T(8,128)S(1)}, f32[64,128]{1,0:T(8,128)S(1)}, f32[512,64]{1,0:T(8,128)S(1)}) custom-call(bf16[64,1024]{1,0:T(8,128)(2,1)S(1)} %bitcast.12, bf16[1,4096]{1,0:T(2,128)(2,1)S(1)} %copy-done.4, bf16[3,4096,512]{2,1,0:T(8,128)(2,1)S(1)} %bitcast.7, ...), custom_call_target="tpu_custom_call" | custom-call | tf_op jit(solution)/shard_map/pallas_call | solution.py:65
  18.9 2.2 %shard_map.65.refs_3_ = bf16[64,512]{1,0:T(8,128)(2,1)S(1)} custom-call(bf16[64,1024]{1,0:T(8,128)(2,1)S(1)} %collective-permute-done.refs_0_, bf16[64,1024]{1,0:T(8,128)(2,1)S(1)} %collective-permute-done.1.refs_1_, bf16[64,1024]{1,0:T(8,128)(2,1)S(1)} %collective-permute-done.2.refs_2_, bf16[1,4096]{1,0:T(2,128)(2,1)S(1)} %copy-done.4, ...), custom_call_target="tpu_custom_call" | custom-call | tf_op jit(solution)/shard_map/pallas_call | solution.py:65
  21.1 3.9 %collective-permute-start.5 = (bf16[64,512]{1,0:T(8,128)(2,1)S(1)}, bf16[64,512]{1,0:T(8,128)(2,1)S(1)}, u32[]{:S(2)}, u32[]{:S(2)}) collective-permute-start(bf16[64,512]{1,0:T(8,128)(2,1)S(1)} %shard_map.65.refs_3_), channel_id=1, source_target_pairs={{0,3},{1,2},{2,1},{3,0},{4,7},{5,6},{6,5},{7,4},{8,11},{9,10},{10,... | collective-permute-start | bytes 196616 | tf_op jit(solution)/shard_map/ppermute | solution.py:46
  25.6 2.0 %collective-permute-done.5.refs_2_ = bf16[64,512]{1,0:T(8,128)(2,1)S(1)} collective-permute-done((bf16[64,512]{1,0:T(8,128)(2,1)S(1)}, bf16[64,512]{1,0:T(8,128)(2,1)S(1)}, u32[]{:S(2)}, u32[]{:S(2)}) %collective-permute-start.5) | collective-permute-done | bytes 65568 | tf_op jit(solution)/shard_map/ppermute | solution.py:46
  27.6 2.5 %collective-permute-done.4.refs_1_ = bf16[64,512]{1,0:T(8,128)(2,1)S(1)} collective-permute-done((bf16[64,512]{1,0:T(8,128)(2,1)S(1)}, bf16[64,512]{1,0:T(8,128)(2,1)S(1)}, u32[]{:S(2)}, u32[]{:S(2)}) %collective-permute-start.4) | collective-permute-done | bytes 65568 | tf_op jit(solution)/shard_map/ppermute | solution.py:46
  32.7 3.4 %collective-permute-done.6.x_ref.refs_5_ = bf16[64,1024]{1,0:T(8,128)(2,1)S(1)} collective-permute-done((bf16[64,1024]{1,0:T(8,128)(2,1)S(1)}, bf16[64,1024]{1,0:T(8,128)(2,1)S(1)}, u32[]{:S(2)}, u32[]{:S(2)}) %collective-permute-start.6) | collective-permute-done | bytes 131104 | tf_op jit(solution)/shard_map/ppermute | solution.py:232
  36.1 2.2 %collective-permute-start.9 = (bf16[64,1024]{1,0:T(8,128)(2,1)S(1)}, bf16[64,1024]{1,0:T(8,128)(2,1)S(1)}, u32[]{:S(2)}, u32[]{:S(2)}) collective-permute-start(bf16[64,1024]{1,0:T(8,128)(2,1)S(1)} %collective-permute-done.6.x_ref.refs_5_), channel_id=1, source_target_pairs={{0,3},{1,2},{2,1},{3,0},{4,7},{5,6},{6,5},{7,4},{8,11},{9,10},{10,... | collective-permute-start | bytes 393224 | tf_op jit(solution)/shard_map/ppermute | solution.py:46
  38.3 2.2 %collective-permute-start.7 = (bf16[64,1024]{1,0:T(8,128)(2,1)S(1)}, bf16[64,1024]{1,0:T(8,128)(2,1)S(1)}, u32[]{:S(2)}, u32[]{:S(2)}) collective-permute-start(bf16[64,1024]{1,0:T(8,128)(2,1)S(1)} %collective-permute-done.6.x_ref.refs_5_), channel_id=1, source_target_pairs={{0,1},{1,0},{2,3},{3,2},{4,5},{5,4},{6,7},{7,6},{8,9},{9,8},{10,11... | collective-permute-start | bytes 393224 | tf_op jit(solution)/shard_map/ppermute | solution.py:46
  41.2 2.7 %collective-permute-done.9.refs_2_ = bf16[64,1024]{1,0:T(8,128)(2,1)S(1)} collective-permute-done((bf16[64,1024]{1,0:T(8,128)(2,1)S(1)}, bf16[64,1024]{1,0:T(8,128)(2,1)S(1)}, u32[]{:S(2)}, u32[]{:S(2)}) %collective-permute-start.9) | collective-permute-done | bytes 131104 | tf_op jit(solution)/shard_map/ppermute | solution.py:46
  43.9 3.6 %collective-permute-done.8.refs_1_ = bf16[64,1024]{1,0:T(8,128)(2,1)S(1)} collective-permute-done((bf16[64,1024]{1,0:T(8,128)(2,1)S(1)}, bf16[64,1024]{1,0:T(8,128)(2,1)S(1)}, u32[]{:S(2)}, u32[]{:S(2)}) %collective-permute-start.8) | collective-permute-done | bytes 131104 | tf_op jit(solution)/shard_map/ppermute | solution.py:46
  47.5 2.2 %shard_map.68.refs_3_ = bf16[64,512]{1,0:T(8,128)(2,1)S(1)} custom-call(bf16[64,1024]{1,0:T(8,128)(2,1)S(1)} %collective-permute-done.7.refs_0_, bf16[64,1024]{1,0:T(8,128)(2,1)S(1)} %collective-permute-done.8.refs_1_, bf16[64,1024]{1,0:T(8,128)(2,1)S(1)} %collective-permute-done.9.refs_2_, bf16[1,4096]{1,0:T(2,128)(2,1)S(1)} %copy-done.4, ...), custom_call_target="tpu_custom_call" | custom-call | tf_op jit(solution)/shard_map/pallas_call | solution.py:65
  49.6 1.8 %collective-permute-start.12 = (bf16[64,512]{1,0:T(8,128)(2,1)S(1)}, bf16[64,512]{1,0:T(8,128)(2,1)S(1)}, u32[]{:S(2)}, u32[]{:S(2)}) collective-permute-start(bf16[64,512]{1,0:T(8,128)(2,1)S(1)} %shard_map.68.refs_3_), channel_id=1, source_target_pairs={{0,3},{1,2},{2,1},{3,0},{4,7},{5,6},{6,5},{7,4},{8,11},{9,10},{10,... | collective-permute-start | bytes 196616 | tf_op jit(solution)/shard_map/ppermute | solution.py:46
  51.4 2.7 %collective-permute-start.10 = (bf16[64,512]{1,0:T(8,128)(2,1)S(1)}, bf16[64,512]{1,0:T(8,128)(2,1)S(1)}, u32[]{:S(2)}, u32[]{:S(2)}) collective-permute-start(bf16[64,512]{1,0:T(8,128)(2,1)S(1)} %shard_map.68.refs_3_), channel_id=1, source_target_pairs={{0,1},{1,0},{2,3},{3,2},{4,5},{5,4},{6,7},{7,6},{8,9},{9,8},{10,11... | collective-permute-start | bytes 196616 | tf_op jit(solution)/shard_map/ppermute | solution.py:46
  59.6 3.4 %collective-permute-done.13.x_ref.refs_5_.refs_6_ = bf16[64,1024]{1,0:T(8,128)(2,1)S(1)} collective-permute-done((bf16[64,1024]{1,0:T(8,128)(2,1)S(1)}, bf16[64,1024]{1,0:T(8,128)(2,1)S(1)}, u32[]{:S(2)}, u32[]{:S(2)}) %collective-permute-start.13) | collective-permute-done | bytes 131104 | tf_op jit(solution)/shard_map/ppermute | solution.py:232
  63.0 1.7 %collective-permute-start.16 = (bf16[64,1024]{1,0:T(8,128)(2,1)S(1)}, bf16[64,1024]{1,0:T(8,128)(2,1)S(1)}, u32[]{:S(2)}, u32[]{:S(2)}) collective-permute-start(bf16[64,1024]{1,0:T(8,128)(2,1)S(1)} %collective-permute-done.13.x_ref.refs_5_.refs_6_), channel_id=1, source_target_pairs={{0,3},{1,2},{2,1},{3,0},{4,7},{5,6},{6,5},{7,4},{8,11},{9,10},{10,... | collective-permute-start | bytes 393224 | tf_op jit(solution)/shard_map/ppermute | solution.py:46
  65.7 1.7 %collective-permute-start.14 = (bf16[64,1024]{1,0:T(8,128)(2,1)S(1)}, bf16[64,1024]{1,0:T(8,128)(2,1)S(1)}, u32[]{:S(2)}, u32[]{:S(2)}) collective-permute-start(bf16[64,1024]{1,0:T(8,128)(2,1)S(1)} %collective-permute-done.13.x_ref.refs_5_.refs_6_), channel_id=1, source_target_pairs={{0,1},{1,0},{2,3},{3,2},{4,5},{5,4},{6,7},{7,6},{8,9},{9,8},{10,11... | collective-permute-start | bytes 393224 | tf_op jit(solution)/shard_map/ppermute | solution.py:46
  68.1 1.9 %collective-permute-done.16.refs_2_ = bf16[64,1024]{1,0:T(8,128)(2,1)S(1)} collective-permute-done((bf16[64,1024]{1,0:T(8,128)(2,1)S(1)}, bf16[64,1024]{1,0:T(8,128)(2,1)S(1)}, u32[]{:S(2)}, u32[]{:S(2)}) %collective-permute-start.16) | collective-permute-done | bytes 131104 | tf_op jit(solution)/shard_map/ppermute | solution.py:46
  70.0 3.5 %collective-permute-done.15.refs_1_ = bf16[64,1024]{1,0:T(8,128)(2,1)S(1)} collective-permute-done((bf16[64,1024]{1,0:T(8,128)(2,1)S(1)}, bf16[64,1024]{1,0:T(8,128)(2,1)S(1)}, u32[]{:S(2)}, u32[]{:S(2)}) %collective-permute-start.15) | collective-permute-done | bytes 131104 | tf_op jit(solution)/shard_map/ppermute | solution.py:46
  73.4 2.2 %shard_map.71.refs_3_ = bf16[64,512]{1,0:T(8,128)(2,1)S(1)} custom-call(bf16[64,1024]{1,0:T(8,128)(2,1)S(1)} %collective-permute-done.14.refs_0_, bf16[64,1024]{1,0:T(8,128)(2,1)S(1)} %collective-permute-done.15.refs_1_, bf16[64,1024]{1,0:T(8,128)(2,1)S(1)} %collective-permute-done.16.refs_2_, bf16[1,4096]{1,0:T(2,128)(2,1)S(1)} %copy-done.4, ...), custom_call_target="tpu_custom_call" | custom-call | tf_op jit(solution)/shard_map/pallas_call | solution.py:65
  75.6 2.1 %collective-permute-start.19 = (bf16[64,512]{1,0:T(8,128)(2,1)S(1)}, bf16[64,512]{1,0:T(8,128)(2,1)S(1)}, u32[]{:S(2)}, u32[]{:S(2)}) collective-permute-start(bf16[64,512]{1,0:T(8,128)(2,1)S(1)} %shard_map.71.refs_3_), channel_id=1, source_target_pairs={{0,3},{1,2},{2,1},{3,0},{4,7},{5,6},{6,5},{7,4},{8,11},{9,10},{10,... | collective-permute-start | bytes 196616 | tf_op jit(solution)/shard_map/ppermute | solution.py:46
  77.7 2.3 %collective-permute-start.17 = (bf16[64,512]{1,0:T(8,128)(2,1)S(1)}, bf16[64,512]{1,0:T(8,128)(2,1)S(1)}, u32[]{:S(2)}, u32[]{:S(2)}) collective-permute-start(bf16[64,512]{1,0:T(8,128)(2,1)S(1)} %shard_map.71.refs_3_), channel_id=1, source_target_pairs={{0,1},{1,0},{2,3},{3,2},{4,5},{5,4},{6,7},{7,6},{8,9},{9,8},{10,11... | collective-permute-start | bytes 196616 | tf_op jit(solution)/shard_map/ppermute | solution.py:46
  (40 shorter events, 19.2 us)
Async XLA Ops:
  0.0 18.9 %collective-permute-start.2 = (bf16[64,1024]{1,0:T(8,128)(2,1)}, bf16[64,1024]{1,0:T(8,128)(2,1)S(1)}, u32[]{:S(2)}, u32[]{:S(2)}) collective-permute-start(bf16[64,1024]{1,0:T(8,128)(2,1)} %bitcast.9), channel_id=1, source_target_pairs={{0,3},{1,2},{2,1},{3,0},{4,7},{5,6},{6,5},{7,4},{8,11},{9,10},{10,... | collective-permute-start | bytes 393224 | tf_op jit(solution)/shard_map/ppermute | solution.py:46
  5.1 13.8 %collective-permute-start.1 = (bf16[64,1024]{1,0:T(8,128)(2,1)}, bf16[64,1024]{1,0:T(8,128)(2,1)S(1)}, u32[]{:S(2)}, u32[]{:S(2)}) collective-permute-start(bf16[64,1024]{1,0:T(8,128)(2,1)} %bitcast.10), channel_id=1, source_target_pairs={{0,2},{1,3},{2,0},{3,1},{4,6},{5,7},{6,4},{7,5},{8,10},{9,11},{10,... | collective-permute-start | bytes 393224 | tf_op jit(solution)/shard_map/ppermute | solution.py:46
  5.1 13.8 %collective-permute-start = (bf16[64,1024]{1,0:T(8,128)(2,1)}, bf16[64,1024]{1,0:T(8,128)(2,1)S(1)}, u32[]{:S(2)}, u32[]{:S(2)}) collective-permute-start(bf16[64,1024]{1,0:T(8,128)(2,1)} %bitcast.11), channel_id=1, source_target_pairs={{0,1},{1,0},{2,3},{3,2},{4,5},{5,4},{6,7},{7,6},{8,9},{9,8},{10,11... | collective-permute-start | bytes 393224 | tf_op jit(solution)/shard_map/ppermute | solution.py:46
  5.6 4.6 %copy-start = (bf16[1,4096,3,512]{3,1,2,0:T(8,128)(2,1)S(1)}, bf16[1,4096,3,512]{3,1,2,0:T(8,128)(2,1)}, u32[]{:S(2)}) copy-start(bf16[1,4096,3,512]{3,1,2,0:T(8,128)(2,1)} %param.7) | copy-start | bytes 37748740
  10.2 2.2 %copy-start.1 = (bf16[1,2048,1024]{2,1,0:T(8,128)(2,1)S(1)}, bf16[1,2048,1024]{2,1,0:T(8,128)(2,1)}, u32[]{:S(2)}) copy-start(bf16[1,2048,1024]{2,1,0:T(8,128)(2,1)} %param.8) | copy-start | bytes 12582916
  12.4 0.9 %copy-start.2 = (bf16[1,64,1024]{2,1,0:T(8,128)(2,1)S(1)}, bf16[1,64,1024]{2,1,0:T(8,128)(2,1)}, u32[]{:S(2)}) copy-start(bf16[1,64,1024]{2,1,0:T(8,128)(2,1)} %param.6) | copy-start | bytes 393220
  15.5 14.8 %copy-start.3 = (bf16[1,64,1024]{2,1,0:T(8,128)(2,1)S(1)}, bf16[1,64,1024]{2,1,0:T(8,128)(2,1)}, u32[]{:S(2)}) copy-start(bf16[1,64,1024]{2,1,0:T(8,128)(2,1)} %param.6) | copy-start | bytes 393220
  21.1 6.5 %collective-permute-start.5 = (bf16[64,512]{1,0:T(8,128)(2,1)S(1)}, bf16[64,512]{1,0:T(8,128)(2,1)S(1)}, u32[]{:S(2)}, u32[]{:S(2)}) collective-permute-start(bf16[64,512]{1,0:T(8,128)(2,1)S(1)} %shard_map.65.refs_3_), channel_id=1, source_target_pairs={{0,3},{1,2},{2,1},{3,0},{4,7},{5,6},{6,5},{7,4},{8,11},{9,10},{10,... | collective-permute-start | bytes 196616 | tf_op jit(solution)/shard_map/ppermute | solution.py:46
  24.9 5.2 %collective-permute-start.4 = (bf16[64,512]{1,0:T(8,128)(2,1)S(1)}, bf16[64,512]{1,0:T(8,128)(2,1)S(1)}, u32[]{:S(2)}, u32[]{:S(2)}) collective-permute-start(bf16[64,512]{1,0:T(8,128)(2,1)S(1)} %shard_map.65.refs_3_), channel_id=1, source_target_pairs={{0,2},{1,3},{2,0},{3,1},{4,6},{5,7},{6,4},{7,5},{8,10},{9,11},{10,... | collective-permute-start | bytes 196616 | tf_op jit(solution)/shard_map/ppermute | solution.py:46
  24.9 5.3 %collective-permute-start.3 = (bf16[64,512]{1,0:T(8,128)(2,1)S(1)}, bf16[64,512]{1,0:T(8,128)(2,1)S(1)}, u32[]{:S(2)}, u32[]{:S(2)}) collective-permute-start(bf16[64,512]{1,0:T(8,128)(2,1)S(1)} %shard_map.65.refs_3_), channel_id=1, source_target_pairs={{0,1},{1,0},{2,3},{3,2},{4,5},{5,4},{6,7},{7,6},{8,9},{9,8},{10,11... | collective-permute-start | bytes 196616 | tf_op jit(solution)/shard_map/ppermute | solution.py:46
  31.1 5.0 %collective-permute-start.6 = (bf16[64,1024]{1,0:T(8,128)(2,1)S(1)}, bf16[64,1024]{1,0:T(8,128)(2,1)S(1)}, u32[]{:S(2)}, u32[]{:S(2)}) collective-permute-start(bf16[64,1024]{1,0:T(8,128)(2,1)S(1)} %shard_map.66), channel_id=1, source_target_pairs={{0,4},{4,0},{1,5},{5,1},{2,6},{6,2},{3,7},{7,3},{8,12},{12,8},{9,1... | collective-permute-start | bytes 393224 | tf_op jit(solution)/shard_map/ppermute | solution.py:232
  36.1 7.8 %collective-permute-start.9 = (bf16[64,1024]{1,0:T(8,128)(2,1)S(1)}, bf16[64,1024]{1,0:T(8,128)(2,1)S(1)}, u32[]{:S(2)}, u32[]{:S(2)}) collective-permute-start(bf16[64,1024]{1,0:T(8,128)(2,1)S(1)} %collective-permute-done.6.x_ref.refs_5_), channel_id=1, source_target_pairs={{0,3},{1,2},{2,1},{3,0},{4,7},{5,6},{6,5},{7,4},{8,11},{9,10},{10,... | collective-permute-start | bytes 393224 | tf_op jit(solution)/shard_map/ppermute | solution.py:46
  38.3 9.2 %collective-permute-start.8 = (bf16[64,1024]{1,0:T(8,128)(2,1)S(1)}, bf16[64,1024]{1,0:T(8,128)(2,1)S(1)}, u32[]{:S(2)}, u32[]{:S(2)}) collective-permute-start(bf16[64,1024]{1,0:T(8,128)(2,1)S(1)} %collective-permute-done.6.x_ref.refs_5_), channel_id=1, source_target_pairs={{0,2},{1,3},{2,0},{3,1},{4,6},{5,7},{6,4},{7,5},{8,10},{9,11},{10,... | collective-permute-start | bytes 393224 | tf_op jit(solution)/shard_map/ppermute | solution.py:46
  38.3 9.2 %collective-permute-start.7 = (bf16[64,1024]{1,0:T(8,128)(2,1)S(1)}, bf16[64,1024]{1,0:T(8,128)(2,1)S(1)}, u32[]{:S(2)}, u32[]{:S(2)}) collective-permute-start(bf16[64,1024]{1,0:T(8,128)(2,1)S(1)} %collective-permute-done.6.x_ref.refs_5_), channel_id=1, source_target_pairs={{0,1},{1,0},{2,3},{3,2},{4,5},{5,4},{6,7},{7,6},{8,9},{9,8},{10,11... | collective-permute-start | bytes 393224 | tf_op jit(solution)/shard_map/ppermute | solution.py:46
  49.6 6.1 %collective-permute-start.12 = (bf16[64,512]{1,0:T(8,128)(2,1)S(1)}, bf16[64,512]{1,0:T(8,128)(2,1)S(1)}, u32[]{:S(2)}, u32[]{:S(2)}) collective-permute-start(bf16[64,512]{1,0:T(8,128)(2,1)S(1)} %shard_map.68.refs_3_), channel_id=1, source_target_pairs={{0,3},{1,2},{2,1},{3,0},{4,7},{5,6},{6,5},{7,4},{8,11},{9,10},{10,... | collective-permute-start | bytes 196616 | tf_op jit(solution)/shard_map/ppermute | solution.py:46
  51.4 5.7 %collective-permute-start.11 = (bf16[64,512]{1,0:T(8,128)(2,1)S(1)}, bf16[64,512]{1,0:T(8,128)(2,1)S(1)}, u32[]{:S(2)}, u32[]{:S(2)}) collective-permute-start(bf16[64,512]{1,0:T(8,128)(2,1)S(1)} %shard_map.68.refs_3_), channel_id=1, source_target_pairs={{0,2},{1,3},{2,0},{3,1},{4,6},{5,7},{6,4},{7,5},{8,10},{9,11},{10,... | collective-permute-start | bytes 196616 | tf_op jit(solution)/shard_map/ppermute | solution.py:46
  51.4 5.7 %collective-permute-start.10 = (bf16[64,512]{1,0:T(8,128)(2,1)S(1)}, bf16[64,512]{1,0:T(8,128)(2,1)S(1)}, u32[]{:S(2)}, u32[]{:S(2)}) collective-permute-start(bf16[64,512]{1,0:T(8,128)(2,1)S(1)} %shard_map.68.refs_3_), channel_id=1, source_target_pairs={{0,1},{1,0},{2,3},{3,2},{4,5},{5,4},{6,7},{7,6},{8,9},{9,8},{10,11... | collective-permute-start | bytes 196616 | tf_op jit(solution)/shard_map/ppermute | solution.py:46
  58.0 5.0 %collective-permute-start.13 = (bf16[64,1024]{1,0:T(8,128)(2,1)S(1)}, bf16[64,1024]{1,0:T(8,128)(2,1)S(1)}, u32[]{:S(2)}, u32[]{:S(2)}) collective-permute-start(bf16[64,1024]{1,0:T(8,128)(2,1)S(1)} %shard_map.69), channel_id=1, source_target_pairs={{0,4},{4,0},{1,5},{5,1},{2,6},{6,2},{3,7},{7,3},{8,12},{12,8},{9,1... | collective-permute-start | bytes 393224 | tf_op jit(solution)/shard_map/ppermute | solution.py:232
  63.0 6.9 %collective-permute-start.16 = (bf16[64,1024]{1,0:T(8,128)(2,1)S(1)}, bf16[64,1024]{1,0:T(8,128)(2,1)S(1)}, u32[]{:S(2)}, u32[]{:S(2)}) collective-permute-start(bf16[64,1024]{1,0:T(8,128)(2,1)S(1)} %collective-permute-done.13.x_ref.refs_5_.refs_6_), channel_id=1, source_target_pairs={{0,3},{1,2},{2,1},{3,0},{4,7},{5,6},{6,5},{7,4},{8,11},{9,10},{10,... | collective-permute-start | bytes 393224 | tf_op jit(solution)/shard_map/ppermute | solution.py:46
  64.8 8.7 %collective-permute-start.15 = (bf16[64,1024]{1,0:T(8,128)(2,1)S(1)}, bf16[64,1024]{1,0:T(8,128)(2,1)S(1)}, u32[]{:S(2)}, u32[]{:S(2)}) collective-permute-start(bf16[64,1024]{1,0:T(8,128)(2,1)S(1)} %collective-permute-done.13.x_ref.refs_5_.refs_6_), channel_id=1, source_target_pairs={{0,2},{1,3},{2,0},{3,1},{4,6},{5,7},{6,4},{7,5},{8,10},{9,11},{10,... | collective-permute-start | bytes 393224 | tf_op jit(solution)/shard_map/ppermute | solution.py:46
  65.7 7.8 %collective-permute-start.14 = (bf16[64,1024]{1,0:T(8,128)(2,1)S(1)}, bf16[64,1024]{1,0:T(8,128)(2,1)S(1)}, u32[]{:S(2)}, u32[]{:S(2)}) collective-permute-start(bf16[64,1024]{1,0:T(8,128)(2,1)S(1)} %collective-permute-done.13.x_ref.refs_5_.refs_6_), channel_id=1, source_target_pairs={{0,1},{1,0},{2,3},{3,2},{4,5},{5,4},{6,7},{7,6},{8,9},{9,8},{10,11... | collective-permute-start | bytes 393224 | tf_op jit(solution)/shard_map/ppermute | solution.py:46
  75.6 6.1 %collective-permute-start.19 = (bf16[64,512]{1,0:T(8,128)(2,1)S(1)}, bf16[64,512]{1,0:T(8,128)(2,1)S(1)}, u32[]{:S(2)}, u32[]{:S(2)}) collective-permute-start(bf16[64,512]{1,0:T(8,128)(2,1)S(1)} %shard_map.71.refs_3_), channel_id=1, source_target_pairs={{0,3},{1,2},{2,1},{3,0},{4,7},{5,6},{6,5},{7,4},{8,11},{9,10},{10,... | collective-permute-start | bytes 196616 | tf_op jit(solution)/shard_map/ppermute | solution.py:46
  77.7 5.4 %collective-permute-start.18 = (bf16[64,512]{1,0:T(8,128)(2,1)S(1)}, bf16[64,512]{1,0:T(8,128)(2,1)S(1)}, u32[]{:S(2)}, u32[]{:S(2)}) collective-permute-start(bf16[64,512]{1,0:T(8,128)(2,1)S(1)} %shard_map.71.refs_3_), channel_id=1, source_target_pairs={{0,2},{1,3},{2,0},{3,1},{4,6},{5,7},{6,4},{7,5},{8,10},{9,11},{10,... | collective-permute-start | bytes 196616 | tf_op jit(solution)/shard_map/ppermute | solution.py:46
  77.7 5.4 %collective-permute-start.17 = (bf16[64,512]{1,0:T(8,128)(2,1)S(1)}, bf16[64,512]{1,0:T(8,128)(2,1)S(1)}, u32[]{:S(2)}, u32[]{:S(2)}) collective-permute-start(bf16[64,512]{1,0:T(8,128)(2,1)S(1)} %shard_map.71.refs_3_), channel_id=1, source_target_pairs={{0,1},{1,0},{2,3},{3,2},{4,5},{5,4},{6,7},{7,6},{8,9},{9,8},{10,11... | collective-permute-start | bytes 196616 | tf_op jit(solution)/shard_map/ppermute | solution.py:46
  (3 other events, 2.2 us)

commit v3 on v2

--- a/solution.py
+++ b/solution.py
@@ -11,6 +11,10 @@
 REACH = 128
 NORM_EPSILON = 0.1
 MOST_DIRECT = 4
+FIRST_ORDER = (1, 3, 2)
+MIX_ORDER = (1, 3, 2)
+REST_ORDER = (1, 3, 2)
+ACROSS = (2,)
 LANES = 128
 F32 = jnp.float32
 BF16 = jnp.bfloat16
@@ -32,25 +36,33 @@
     return (upper_side + np.where(distance < exact_count, distance, far_bucket)).astype(np.int32)
 
 
-def swap_masks(peers):
+def swap_masks(peers, order=MIX_ORDER):
     if peers & (peers - 1) or peers > MOST_DIRECT:
         return None
-    return sorted(range(1, peers), key=lambda mask: (bin(mask).count("1"), mask))
-
-
-def from_peers(x, axis):
-    peers = lax.axis_size(axis)
-    masks = swap_masks(peers)
+    return [mask for mask in order if mask < peers]
+
+
+def swapped(x, mask, across=False):
+    sections, peers = lax.axis_size("section"), lax.axis_size("mp")
+    pairs = [
+        (s * peers + i, ((s ^ 1) if across else s) * peers + (i ^ mask))
+        for s in range(sections)
+        for i in range(peers)
+    ]
+    return lax.ppermute(x, ("section", "mp"), pairs)
+
+
+def from_peers(x, order=MIX_ORDER):
+    masks = swap_masks(lax.axis_size("mp"), order)
     if masks is None:
-        return [lax.all_gather(x, axis, axis=0, tiled=False)]
-    return [lax.ppermute(x, axis, [(i, i ^ mask) for i in range(peers)]) for mask in masks]
-
-
-def peer_blocks(refs, axis):
-    peers = lax.axis_size(axis)
-    me = lax.axis_index(axis)
-    masks = swap_masks(peers)
-    if masks is None:
+        return [(None, lax.all_gather(x, "mp", axis=0, tiled=False))]
+    return [(mask, swapped(x, mask)) for mask in masks]
+
+
+def peer_blocks(masks, refs):
+    peers = lax.axis_size("mp")
+    me = lax.axis_index("mp")
+    if masks == [None]:
         turned = [lax.rem(me + step, peers) for step in range(1, peers)]
         return [(peer, refs[0][peer]) for peer in turned]
     return [(me ^ mask, ref[...]) for mask, ref in zip(masks, refs)]
@@ -92,21 +104,23 @@
     squares_ref[...] = add_part(peer, block, gain_ref, weight_ref, total_ref, squares)
 
 
-def load_kernel(x_ref, gain_ref, qkv_ref, out_ref, table_ref, grid_ref,
-                held_qkv, held_out, total_ref, squares_ref, bias_ref, sems):
+def load_kernel(x_in, gain_in, qkv_in, out_in, table_ref, grid_in,
+                x_ref, gain_ref, held_qkv, held_out, total_ref, squares_ref, bias_ref,
+                grid_ref, sems):
     peers = lax.axis_size("mp")
     me = lax.axis_index("mp")
-    width = x_ref.shape[1]
-    copies = []
+    width = x_in.shape[1]
+    pairs = [(grid_in, grid_ref), (x_in, x_ref), (gain_in, gain_ref)]
     for step in range(peers):
         rows = rows_of(lax.rem(me + step, peers), width)
-        copies.append(pltpu.make_async_copy(
-            qkv_ref.at[:, rows, :], held_qkv.at[:, rows, :], sems.at[step]))
-    copies.append(pltpu.make_async_copy(out_ref, held_out, sems.at[peers]))
+        pairs.append((qkv_in.at[:, rows, :], held_qkv.at[:, rows, :]))
+    pairs.append((out_in, held_out))
+    copies = [pltpu.make_async_copy(a, b, sems.at[i]) for i, (a, b) in enumerate(pairs)]
     for copy in copies:
         copy.start()
     heads, buckets = table_ref.shape
     length = grid_ref.shape[0]
+    copies[0].wait()
 
     def one_head(head, carry):
         grid = grid_ref[...]
@@ -117,9 +131,10 @@
         return carry
 
     lax.fori_loop(0, heads, one_head, 0)
-    copies[0].wait()
+    for copy in copies[1:4]:
+        copy.wait()
     own_part(me, x_ref[...], gain_ref, held_qkv, total_ref, squares_ref)
-    for copy in copies[1:]:
+    for copy in copies[4:]:
         copy.wait()
 
 
@@ -127,11 +142,22 @@
     own_part(lax.axis_index("mp"), x_ref[...], gain_ref, held_qkv, total_ref, squares_ref)
 
 
-def attend_kernel(head_size, model_width, *refs):
-    *peer_refs, gain_ref, held_qkv, partial_ref, partial_squares, bias_ref, mix_ref, total_ref = refs
+def add_kernel(masks, *refs):
+    peer_refs = refs[: len(masks)]
+    gain_ref, held_qkv, partial_ref, partial_squares, total_ref, squares_ref = refs[len(masks):]
     total_ref[...] = partial_ref[...]
     squares = partial_squares[...]
-    for peer, block in peer_blocks(peer_refs, "mp"):
+    for peer, block in peer_blocks(masks, peer_refs):
+        squares = add_part(peer, block, gain_ref, held_qkv, total_ref, squares)
+    squares_ref[...] = squares
+
+
+def attend_kernel(masks, head_size, model_width, *refs):
+    peer_refs = refs[: len(masks)]
+    gain_ref, held_qkv, partial_ref, partial_squares, bias_ref, mix_ref, total_ref = refs[len(masks):]
+    total_ref[...] = partial_ref[...]
+    squares = partial_squares[...]
+    for peer, block in peer_blocks(masks, peer_refs):
         squares = add_part(peer, block, gain_ref, held_qkv, total_ref, squares)
     mean_square = jnp.sum(squares, axis=1, keepdims=True) / model_width
     row_scale = lax.rsqrt(mean_square + NORM_EPSILON)
@@ -160,14 +186,24 @@
         mix_ref[:, lanes] = mix.astype(BF16)
 
 
-def out_kernel(keep_section, *refs):
-    *peer_refs, own_ref, held_out, stream_ref, kept_ref, result_ref = refs
-    local_qkv = own_ref.shape[1]
-    total = stream_ref[...].astype(F32)
-    blocks = [(lax.axis_index("mp"), own_ref[...])] + peer_blocks(peer_refs, "mp")
+def out_part_kernel(masks, *refs):
+    peer_refs = refs[: len(masks)]
+    own_ref, held_out, stream_ref, total_ref = refs[len(masks):]
+    total_ref[...] = add_mixes(stream_ref[...].astype(F32), [(lax.axis_index("mp"), own_ref[...])]
+                               + peer_blocks(masks, peer_refs), held_out)
+
+
+def add_mixes(total, blocks, held_out):
     for peer, block in blocks:
-        part = held_out[rows_of(peer, local_qkv), :]
+        part = held_out[rows_of(peer, block.shape[1]), :]
         total += jnp.dot(block, part, preferred_element_type=F32)
+    return total
+
+
+def out_kernel(masks, keep_section, *refs):
+    peer_refs = refs[: len(masks)]
+    held_out, partial_ref, kept_ref, result_ref = refs[len(masks):]
+    total = add_mixes(partial_ref[...], peer_blocks(masks, peer_refs), held_out)
     result = total.astype(BF16)
     if keep_section is not None:
         result = jnp.where(lax.axis_index("section") == keep_section, kept_ref[...], result)
@@ -196,57 +232,93 @@
 
     total = VMEM((3, length, local_qkv), F32)
     squares = VMEM((length, LANES), F32)
-    held = {}
-
-    def attend(section_in, keep_section, kept):
-        others = from_peers(section_in, "mp")
-        if not held:
-            vm = pl.BlockSpec(memory_space=VMEM)
-            hbm = pl.BlockSpec(memory_space=pltpu.HBM)
-            sm = pl.BlockSpec(memory_space=pltpu.SMEM)
-            bias = VMEM((local_heads * length, length), F32)
-            held["qkv"], held["out"], part, part_squares, held["bias"] = call(
-                load_kernel,
-                [VMEM(weights_qkv.shape, BF16), VMEM(weights_out.shape, BF16), total, squares, bias],
-                section_in, norm_gain, weights_qkv, weights_out, position_bias, bucket_grid,
-                specs=[vm, vm, hbm, hbm, sm, vm],
-                scratch=[pltpu.SemaphoreType.DMA((peers + 1,))],
-            )
-        else:
-            part, part_squares = call(
-                own_kernel, [total, squares], section_in, norm_gain, held["qkv"])
-        mix = call(
-            lambda *refs: attend_kernel(head_size, model_width, *refs),
+    raw = micro_inputs[0]
+
+    def stay(x):
+        return pltpu.with_memory_space_constraint(x, pltpu.HBM)
+
+    def load():
+        vm = pl.BlockSpec(memory_space=VMEM)
+        hbm = pl.BlockSpec(memory_space=pltpu.HBM)
+        sm = pl.BlockSpec(memory_space=pltpu.SMEM)
+        return call(
+            load_kernel,
+            [
+                VMEM(raw.shape, BF16), VMEM(norm_gain.shape, BF16),
+                VMEM(weights_qkv.shape, BF16), VMEM(weights_out.shape, BF16),
+                total, squares, VMEM((local_heads * length, length), F32),
+            ],
+            stay(raw), stay(norm_gain), stay(weights_qkv), stay(weights_out),
+            position_bias, stay(bucket_grid),
+            specs=[hbm, hbm, hbm, hbm, sm, hbm],
+            scratch=[VMEM((length, length), jnp.int32), pltpu.SemaphoreType.DMA((peers + 4,))],
+        )
+
+    def add_own(section_in):
+        return call(own_kernel, [total, squares], section_in, gain, held_qkv)
+
+    def attend(others, parts):
+        for early in others[:-1]:
+            masks = [early[0]]
+            parts = call(
+                lambda *refs: add_kernel(masks, *refs), [total, squares],
+                early[1], gain, held_qkv, *parts)
+        late = others[-1:]
+        masks = [mask for mask, block in late]
+        return call(
+            lambda *refs: attend_kernel(masks, head_size, model_width, *refs),
             [VMEM((length, local_qkv), BF16)],
-            *others, norm_gain, held["qkv"], part, part_squares, held["bias"],
+            *[block for mask, block in late], gain, held_qkv, *parts, bias,
             scratch=[total],
         )[0]
-        mixes = from_peers(mix, "mp")
+
+    def project(mixes, mix, stream, keep_section=None, kept=None):
+        early, late = mixes[:-2], mixes[-2:]
+        early_masks = [mask for mask, block in early]
+        late_masks = [mask for mask, block in late]
+        partial = call(
+            lambda *refs: out_part_kernel(early_masks, *refs),
+            [VMEM(stream.shape, F32)],
+            *[block for mask, block in early], mix, held_out, stream,
+        )[0]
         return call(
-            lambda *refs: out_kernel(keep_section, *refs),
-            [VMEM(section_in.shape, BF16)],
-            *mixes, mix, held["out"], section_in, kept,
+            lambda *refs: out_kernel(late_masks, keep_section, *refs),
+            [VMEM(stream.shape, BF16)],
+            *[block for mask, block in late], held_out, partial, stream if kept is None else kept,
         )[0]
+
+    def layer(section_in, others, parts=None, keep_section=None, kept=None):
+        mix = attend(others, parts or add_own(section_in))
+        return project(from_peers(mix), mix, section_in, keep_section, kept)
+
+    def handed_on(out):
+        section_in = swapped(out, 0, across=True)
+        early = [mask for mask in ACROSS if mask < peers]
+        others = [(mask, swapped(out, mask, across=True)) for mask in early]
+        others += [(mask, swapped(section_in, mask)) for mask in swap_masks(peers, REST_ORDER) if mask not in early]
+        return section_in, others
 
     def rotated(x, by):
         return lax.ppermute(x, "section", [(i, (i + by) % sections) for i in range(sections)])
 
-    raw = micro_inputs[0]
-    if sections == 2:
-        handed = rotated(attend(raw, 1, raw), 1)
-        finished = rotated(attend(handed, None, raw), 1)
-        return attend(finished, 0, finished)[None]
+    others = from_peers(raw, FIRST_ORDER)
+    current, gain, held_qkv, held_out, *parts, bias = load()
+    if sections == 2 and swap_masks(peers):
+        current, others = handed_on(layer(current, others, parts, 1, current))
+        current, others = handed_on(layer(current, others))
+        return layer(current, others, None, 0, current)[None]
     ticks = 2 * sections - 1
-    current = raw
-    result = raw
+    result = current
     for tick in range(ticks):
         if tick + 1 < sections:
             raw = rotated(raw, -1)
-        out = attend(current, None, current)
+        out = layer(current, others, parts)
+        parts = None
         done = tick - (sections - 1)
         if tick + 1 < ticks:
             sent = rotated(out, 1)
             current = pick(0, raw, sent)
+            others = from_peers(current)
         if done >= 0:
             owned = rotated(out, done + 1) if done + 1 < sections else out
             result = pick(done, owned, result)

time: 85 us -> 76.2 us (0.90)
  local copies, waits for them, and re-layouts: 10.5 us -> 1.34 us
  starting transfers between devices: 30.9 us -> 24.7 us
  Pallas kernels: 13.7 us -> 18.1 us
  waiting for transfers between devices: 29.4 us -> 31.7 us
    unnamed x15 -> x3, local copies, waits for them, and re-layouts: 10.5 us -> 1.34 us
    ppermute x20, starting transfers between devices: 30.9 us -> 24.7 us  [swapped(): return lax.ppermute(x, ('section', 'mp'), pairs)]
    pallas_call x9 -> x18, Pallas kernels: 13.7 us -> 18.1 us  [call(): pl.pallas_call(body, in_specs=specs, out_specs=tuple((pl.BlockSpec(memory...]
    ppermute x20, waiting for transfers between devices: 29.4 us -> 31.7 us  [swapped(): return lax.ppermute(x, ('section', 'mp'), pairs)]
  transfers between devices with their start and end apart: 20 -> 20, of which waited for: 13 -> 16; matrix products, arithmetic and copies ran while one was open for 0% -> 0% of each run, Pallas kernels for 6% -> 18%
where the time goes in v3:
time: 76.2 us; the launch traced here: 76 us
  waiting for transfers between devices  31.7 us (42%)
  starting transfers between devices  24.7 us (32%)
  Pallas kernels  18.1 us (24%)
  local copies, waits for them, and re-layouts  1.34 us (2%)
    ppermute x20, waiting for transfers between devices, swapped(): return lax.ppermute(x, ('section', 'mp'), pairs)  31.7 us
    ppermute x20, starting transfers between devices, swapped(): return lax.ppermute(x, ('section', 'mp'), pairs)  24.7 us
    pallas_call x18, Pallas kernels, call(): pl.pallas_call(body, in_specs=specs, out_specs=tuple((pl.BlockSpec(memory...  18.1 us
  transfers between devices with their start and end apart: 20, of which 16 were waited for; matrix products, arithmetic and copies ran while one was open for 0% of the time, Pallas kernels for 18%

profile of v3, /device:TPU:0, one launch (start us, length us, event | category | flops | bytes accessed | tf_op | source)
XLA Modules:
  0.0 76.0 jit_solution(3614730412680287393)
XLA Ops:
  0.0 3.1 %collective-permute-start.2 = (bf16[64,1024]{1,0:T(8,128)(2,1)}, bf16[64,1024]{1,0:T(8,128)(2,1)S(1)}, u32[]{:S(2)}, u32[]{:S(2)}) collective-permute-start(bf16[64,1024]{1,0:T(8,128)(2,1)} %bitcast.9), channel_id=1, source_target_pairs={{0,1},{1,0},{2,3},{3,2},{4,5},{5,4},{6,7},{7,6},{8,9},{9,8},{10,11... | collective-permute-start | bytes 393224 | tf_op jit(solution)/shard_map/ppermute | solution.py:52
  3.1 2.5 %collective-permute-start.1 = (bf16[64,1024]{1,0:T(8,128)(2,1)}, bf16[64,1024]{1,0:T(8,128)(2,1)S(1)}, u32[]{:S(2)}, u32[]{:S(2)}) collective-permute-start(bf16[64,1024]{1,0:T(8,128)(2,1)} %bitcast.10), channel_id=1, source_target_pairs={{0,3},{1,2},{2,1},{3,0},{4,7},{5,6},{6,5},{7,4},{8,11},{9,10},{10,... | collective-permute-start | bytes 393224 | tf_op jit(solution)/shard_map/ppermute | solution.py:52
  6.3 6.6 %shard_map.64 = (bf16[64,1024]{1,0:T(8,128)(2,1)S(1)}, bf16[1,4096]{1,0:T(2,128)(2,1)S(1)}, bf16[3,4096,512]{2,1,0:T(8,128)(2,1)S(1)}, bf16[2048,1024]{1,0:T(8,1...) custom-call(bf16[64,1024]{1,0:T(8,128)(2,1)} %bitcast.12, ...), custom_call_target="tpu_custom_call" | custom-call | tf_op jit(solution)/shard_map/pallas_call | solution.py:77
  14.4 3.2 %collective-permute-done.refs_0_ = bf16[64,1024]{1,0:T(8,128)(2,1)S(1)} collective-permute-done((bf16[64,1024]{1,0:T(8,128)(2,1)}, bf16[64,1024]{1,0:T(8,128)(2,1)S(1)}, u32[]{:S(2)}, u32[]{:S(2)}) %collective-permute-start) | collective-permute-done | bytes 131104 | tf_op jit(solution)/shard_map/ppermute | solution.py:52
  18.7 2.7 %collective-permute-start.3 = (bf16[64,512]{1,0:T(8,128)(2,1)S(1)}, bf16[64,512]{1,0:T(8,128)(2,1)S(1)}, u32[]{:S(2)}, u32[]{:S(2)}) collective-permute-start(bf16[64,512]{1,0:T(8,128)(2,1)S(1)} %shard_map.67.refs_1_), channel_id=1, source_target_pairs={{0,3},{1,2},{2,1},{3,0},{4,7},{5,6},{6,5},{7,4},{8,11},{9,10},{10,... | collective-permute-start | bytes 196616 | tf_op jit(solution)/shard_map/ppermute | solution.py:52
  22.1 1.6 %collective-permute-done.5.refs_0_ = bf16[64,512]{1,0:T(8,128)(2,1)S(1)} collective-permute-done((bf16[64,512]{1,0:T(8,128)(2,1)S(1)}, bf16[64,512]{1,0:T(8,128)(2,1)S(1)}, u32[]{:S(2)}, u32[]{:S(2)}) %collective-permute-start.5) | collective-permute-done | bytes 65568 | tf_op jit(solution)/shard_map/ppermute | solution.py:52
  25.3 2.5 %collective-permute-done.4.refs_1_ = bf16[64,512]{1,0:T(8,128)(2,1)S(1)} collective-permute-done((bf16[64,512]{1,0:T(8,128)(2,1)S(1)}, bf16[64,512]{1,0:T(8,128)(2,1)S(1)}, u32[]{:S(2)}, u32[]{:S(2)}) %collective-permute-start.4) | collective-permute-done | bytes 65568 | tf_op jit(solution)/shard_map/ppermute | solution.py:52
  28.3 1.6 %collective-permute-start.6 = (bf16[64,1024]{1,0:T(8,128)(2,1)S(1)}, bf16[64,1024]{1,0:T(8,128)(2,1)S(1)}, u32[]{:S(2)}, u32[]{:S(2)}) collective-permute-start(bf16[64,1024]{1,0:T(8,128)(2,1)S(1)} %shard_map.69), channel_id=1, source_target_pairs={{0,4},{1,5},{2,6},{3,7},{4,0},{5,1},{6,2},{7,3},{8,12},{9,13},{10,... | collective-permute-start | bytes 393224 | tf_op jit(solution)/shard_map/ppermute | solution.py:52
  30.1 4.6 %collective-permute-done.6.x_ref.refs_3_.refs_4_ = bf16[64,1024]{1,0:T(8,128)(2,1)S(1)} collective-permute-done((bf16[64,1024]{1,0:T(8,128)(2,1)S(1)}, bf16[64,1024]{1,0:T(8,128)(2,1)S(1)}, u32[]{:S(2)}, u32[]{:S(2)}) %collective-permute-start.6) | collective-permute-done | bytes 131104 | tf_op jit(solution)/shard_map/ppermute | solution.py:52
  34.7 1.9 %collective-permute-start.7 = (bf16[64,1024]{1,0:T(8,128)(2,1)S(1)}, bf16[64,1024]{1,0:T(8,128)(2,1)S(1)}, u32[]{:S(2)}, u32[]{:S(2)}) collective-permute-start(bf16[64,1024]{1,0:T(8,128)(2,1)S(1)} %collective-permute-done.6.x_ref.refs_3_.refs_4_), channel_id=1, source_target_pairs={{0,3},{1,2},{2,1},{3,0},{4,7},{5,6},{6,5},{7,4},{8,11},{9,10},{10,... | collective-permute-start | bytes 393224 | tf_op jit(solution)/shard_map/ppermute | solution.py:52
  37.3 3.2 %collective-permute-done.9.refs_0_ = bf16[64,1024]{1,0:T(8,128)(2,1)S(1)} collective-permute-done((bf16[64,1024]{1,0:T(8,128)(2,1)S(1)}, bf16[64,1024]{1,0:T(8,128)(2,1)S(1)}, u32[]{:S(2)}, u32[]{:S(2)}) %collective-permute-start.9) | collective-permute-done | bytes 131104 | tf_op jit(solution)/shard_map/ppermute | solution.py:52
  42.3 1.1 %shard_map.73.refs_1_ = bf16[64,512]{1,0:T(8,128)(2,1)S(1)} custom-call(bf16[64,1024]{1,0:T(8,128)(2,1)S(1)} %collective-permute-done.7.refs_0_, bf16[1,4096]{1,0:T(2,128)(2,1)S(1)} %get-tuple-element.28.refs_1_.gain_ref, bf16[3,4096,512]{2,1,0:T(8,128)(2,1)S(1)} %get-tuple-element.29.refs_2_.held_qkv, f32[3,64,512]{2,1,0:T(8,128)S(1)} %get-tuple-element.43.refs_3_, ...), custom_call_target="tpu_custom_call" | custom-call | tf_op jit(solution)/shard_map/pallas_call | solution.py:77
  44.2 1.9 %collective-permute-start.10 = (bf16[64,512]{1,0:T(8,128)(2,1)S(1)}, bf16[64,512]{1,0:T(8,128)(2,1)S(1)}, u32[]{:S(2)}, u32[]{:S(2)}) collective-permute-start(bf16[64,512]{1,0:T(8,128)(2,1)S(1)} %shard_map.73.refs_1_), channel_id=1, source_target_pairs={{0,3},{1,2},{2,1},{3,0},{4,7},{5,6},{6,5},{7,4},{8,11},{9,10},{10,... | collective-permute-start | bytes 196616 | tf_op jit(solution)/shard_map/ppermute | solution.py:52
  46.9 1.2 %collective-permute-done.12.refs_0_ = bf16[64,512]{1,0:T(8,128)(2,1)S(1)} collective-permute-done((bf16[64,512]{1,0:T(8,128)(2,1)S(1)}, bf16[64,512]{1,0:T(8,128)(2,1)S(1)}, u32[]{:S(2)}, u32[]{:S(2)}) %collective-permute-start.12) | collective-permute-done | bytes 65568 | tf_op jit(solution)/shard_map/ppermute | solution.py:52
  48.6 1.7 %collective-permute-done.10.refs_0_ = bf16[64,512]{1,0:T(8,128)(2,1)S(1)} collective-permute-done((bf16[64,512]{1,0:T(8,128)(2,1)S(1)}, bf16[64,512]{1,0:T(8,128)(2,1)S(1)}, u32[]{:S(2)}, u32[]{:S(2)}) %collective-permute-start.10) | collective-permute-done | bytes 65568 | tf_op jit(solution)/shard_map/ppermute | solution.py:52
  50.3 1.4 %collective-permute-done.11.refs_1_ = bf16[64,512]{1,0:T(8,128)(2,1)S(1)} collective-permute-done((bf16[64,512]{1,0:T(8,128)(2,1)S(1)}, bf16[64,512]{1,0:T(8,128)(2,1)S(1)}, u32[]{:S(2)}, u32[]{:S(2)}) %collective-permute-start.11) | collective-permute-done | bytes 65568 | tf_op jit(solution)/shard_map/ppermute | solution.py:52
  52.2 1.6 %collective-permute-start.13 = (bf16[64,1024]{1,0:T(8,128)(2,1)S(1)}, bf16[64,1024]{1,0:T(8,128)(2,1)S(1)}, u32[]{:S(2)}, u32[]{:S(2)}) collective-permute-start(bf16[64,1024]{1,0:T(8,128)(2,1)S(1)} %shard_map.75), channel_id=1, source_target_pairs={{0,4},{1,5},{2,6},{3,7},{4,0},{5,1},{6,2},{7,3},{8,12},{9,13},{10,... | collective-permute-start | bytes 393224 | tf_op jit(solution)/shard_map/ppermute | solution.py:52
  54.2 3.0 %collective-permute-done.13.x_ref.refs_3_.refs_4_ = bf16[64,1024]{1,0:T(8,128)(2,1)S(1)} collective-permute-done((bf16[64,1024]{1,0:T(8,128)(2,1)S(1)}, bf16[64,1024]{1,0:T(8,128)(2,1)S(1)}, u32[]{:S(2)}, u32[]{:S(2)}) %collective-permute-start.13) | collective-permute-done | bytes 131104 | tf_op jit(solution)/shard_map/ppermute | solution.py:52
  57.2 2.0 %collective-permute-start.14 = (bf16[64,1024]{1,0:T(8,128)(2,1)S(1)}, bf16[64,1024]{1,0:T(8,128)(2,1)S(1)}, u32[]{:S(2)}, u32[]{:S(2)}) collective-permute-start(bf16[64,1024]{1,0:T(8,128)(2,1)S(1)} %collective-permute-done.13.x_ref.refs_3_.refs_4_), channel_id=1, source_target_pairs={{0,3},{1,2},{2,1},{3,0},{4,7},{5,6},{6,5},{7,4},{8,11},{9,10},{10,... | collective-permute-start | bytes 393224 | tf_op jit(solution)/shard_map/ppermute | solution.py:52
  59.9 2.3 %collective-permute-done.16.refs_0_ = bf16[64,1024]{1,0:T(8,128)(2,1)S(1)} collective-permute-done((bf16[64,1024]{1,0:T(8,128)(2,1)S(1)}, bf16[64,1024]{1,0:T(8,128)(2,1)S(1)}, u32[]{:S(2)}, u32[]{:S(2)}) %collective-permute-start.16) | collective-permute-done | bytes 131104 | tf_op jit(solution)/shard_map/ppermute | solution.py:52
  65.2 2.2 %collective-permute-start.19 = (bf16[64,512]{1,0:T(8,128)(2,1)S(1)}, bf16[64,512]{1,0:T(8,128)(2,1)S(1)}, u32[]{:S(2)}, u32[]{:S(2)}) collective-permute-start(bf16[64,512]{1,0:T(8,128)(2,1)S(1)} %shard_map.79.refs_1_), channel_id=1, source_target_pairs={{0,1},{1,0},{2,3},{3,2},{4,5},{5,4},{6,7},{7,6},{8,9},{9,8},{10,11... | collective-permute-start | bytes 196616 | tf_op jit(solution)/shard_map/ppermute | solution.py:52
  67.4 2.1 %collective-permute-start.17 = (bf16[64,512]{1,0:T(8,128)(2,1)S(1)}, bf16[64,512]{1,0:T(8,128)(2,1)S(1)}, u32[]{:S(2)}, u32[]{:S(2)}) collective-permute-start(bf16[64,512]{1,0:T(8,128)(2,1)S(1)} %shard_map.79.refs_1_), channel_id=1, source_target_pairs={{0,3},{1,2},{2,1},{3,0},{4,7},{5,6},{6,5},{7,4},{8,11},{9,10},{10,... | collective-permute-start | bytes 196616 | tf_op jit(solution)/shard_map/ppermute | solution.py:52
  70.1 3.3 %collective-permute-done.17.refs_0_ = bf16[64,512]{1,0:T(8,128)(2,1)S(1)} collective-permute-done((bf16[64,512]{1,0:T(8,128)(2,1)S(1)}, bf16[64,512]{1,0:T(8,128)(2,1)S(1)}, u32[]{:S(2)}, u32[]{:S(2)}) %collective-permute-start.17) | collective-permute-done | bytes 65568 | tf_op jit(solution)/shard_map/ppermute | solution.py:52
  73.4 1.4 %collective-permute-done.18.refs_1_ = bf16[64,512]{1,0:T(8,128)(2,1)S(1)} collective-permute-done((bf16[64,512]{1,0:T(8,128)(2,1)S(1)}, bf16[64,512]{1,0:T(8,128)(2,1)S(1)}, u32[]{:S(2)}, u32[]{:S(2)}) %collective-permute-start.18) | collective-permute-done | bytes 65568 | tf_op jit(solution)/shard_map/ppermute | solution.py:52
  (37 shorter events, 17.4 us)
Async XLA Ops:
  0.0 13.0 %collective-permute-start.2 = (bf16[64,1024]{1,0:T(8,128)(2,1)}, bf16[64,1024]{1,0:T(8,128)(2,1)S(1)}, u32[]{:S(2)}, u32[]{:S(2)}) collective-permute-start(bf16[64,1024]{1,0:T(8,128)(2,1)} %bitcast.9), channel_id=1, source_target_pairs={{0,1},{1,0},{2,3},{3,2},{4,5},{5,4},{6,7},{7,6},{8,9},{9,8},{10,11... | collective-permute-start | bytes 393224 | tf_op jit(solution)/shard_map/ppermute | solution.py:52
  3.1 10.6 %collective-permute-start.1 = (bf16[64,1024]{1,0:T(8,128)(2,1)}, bf16[64,1024]{1,0:T(8,128)(2,1)S(1)}, u32[]{:S(2)}, u32[]{:S(2)}) collective-permute-start(bf16[64,1024]{1,0:T(8,128)(2,1)} %bitcast.10), channel_id=1, source_target_pairs={{0,3},{1,2},{2,1},{3,0},{4,7},{5,6},{6,5},{7,4},{8,11},{9,10},{10,... | collective-permute-start | bytes 393224 | tf_op jit(solution)/shard_map/ppermute | solution.py:52
  5.5 12.0 %collective-permute-start = (bf16[64,1024]{1,0:T(8,128)(2,1)}, bf16[64,1024]{1,0:T(8,128)(2,1)S(1)}, u32[]{:S(2)}, u32[]{:S(2)}) collective-permute-start(bf16[64,1024]{1,0:T(8,128)(2,1)} %bitcast.11), channel_id=1, source_target_pairs={{0,2},{1,3},{2,0},{3,1},{4,6},{5,7},{6,4},{7,5},{8,10},{9,11},{10,... | collective-permute-start | bytes 393224 | tf_op jit(solution)/shard_map/ppermute | solution.py:52
  5.6 0.7 copy-start
  18.6 5.2 %collective-permute-start.5 = (bf16[64,512]{1,0:T(8,128)(2,1)S(1)}, bf16[64,512]{1,0:T(8,128)(2,1)S(1)}, u32[]{:S(2)}, u32[]{:S(2)}) collective-permute-start(bf16[64,512]{1,0:T(8,128)(2,1)S(1)} %shard_map.67.refs_1_), channel_id=1, source_target_pairs={{0,1},{1,0},{2,3},{3,2},{4,5},{5,4},{6,7},{7,6},{8,9},{9,8},{10,11... | collective-permute-start | bytes 196616 | tf_op jit(solution)/shard_map/ppermute | solution.py:52
  18.7 6.6 %collective-permute-start.3 = (bf16[64,512]{1,0:T(8,128)(2,1)S(1)}, bf16[64,512]{1,0:T(8,128)(2,1)S(1)}, u32[]{:S(2)}, u32[]{:S(2)}) collective-permute-start(bf16[64,512]{1,0:T(8,128)(2,1)S(1)} %shard_map.67.refs_1_), channel_id=1, source_target_pairs={{0,3},{1,2},{2,1},{3,0},{4,7},{5,6},{6,5},{7,4},{8,11},{9,10},{10,... | collective-permute-start | bytes 196616 | tf_op jit(solution)/shard_map/ppermute | solution.py:52
  21.3 6.4 %collective-permute-start.4 = (bf16[64,512]{1,0:T(8,128)(2,1)S(1)}, bf16[64,512]{1,0:T(8,128)(2,1)S(1)}, u32[]{:S(2)}, u32[]{:S(2)}) collective-permute-start(bf16[64,512]{1,0:T(8,128)(2,1)S(1)} %shard_map.67.refs_1_), channel_id=1, source_target_pairs={{0,2},{1,3},{2,0},{3,1},{4,6},{5,7},{6,4},{7,5},{8,10},{9,11},{10,... | collective-permute-start | bytes 196616 | tf_op jit(solution)/shard_map/ppermute | solution.py:52
  28.3 6.4 %collective-permute-start.6 = (bf16[64,1024]{1,0:T(8,128)(2,1)S(1)}, bf16[64,1024]{1,0:T(8,128)(2,1)S(1)}, u32[]{:S(2)}, u32[]{:S(2)}) collective-permute-start(bf16[64,1024]{1,0:T(8,128)(2,1)S(1)} %shard_map.69), channel_id=1, source_target_pairs={{0,4},{1,5},{2,6},{3,7},{4,0},{5,1},{6,2},{7,3},{8,12},{9,13},{10,... | collective-permute-start | bytes 393224 | tf_op jit(solution)/shard_map/ppermute | solution.py:52
  29.8 10.6 %collective-permute-start.9 = (bf16[64,1024]{1,0:T(8,128)(2,1)S(1)}, bf16[64,1024]{1,0:T(8,128)(2,1)S(1)}, u32[]{:S(2)}, u32[]{:S(2)}) collective-permute-start(bf16[64,1024]{1,0:T(8,128)(2,1)S(1)} %shard_map.69), channel_id=1, source_target_pairs={{0,6},{1,7},{2,4},{3,5},{4,2},{5,3},{6,0},{7,1},{8,14},{9,15},{10,... | collective-permute-start | bytes 393224 | tf_op jit(solution)/shard_map/ppermute | solution.py:52
  34.7 6.9 %collective-permute-start.8 = (bf16[64,1024]{1,0:T(8,128)(2,1)S(1)}, bf16[64,1024]{1,0:T(8,128)(2,1)S(1)}, u32[]{:S(2)}, u32[]{:S(2)}) collective-permute-start(bf16[64,1024]{1,0:T(8,128)(2,1)S(1)} %collective-permute-done.6.x_ref.refs_3_.refs_4_), channel_id=1, source_target_pairs={{0,1},{1,0},{2,3},{3,2},{4,5},{5,4},{6,7},{7,6},{8,9},{9,8},{10,11... | collective-permute-start | bytes 393224 | tf_op jit(solution)/shard_map/ppermute | solution.py:52
  34.7 7.6 %collective-permute-start.7 = (bf16[64,1024]{1,0:T(8,128)(2,1)S(1)}, bf16[64,1024]{1,0:T(8,128)(2,1)S(1)}, u32[]{:S(2)}, u32[]{:S(2)}) collective-permute-start(bf16[64,1024]{1,0:T(8,128)(2,1)S(1)} %collective-permute-done.6.x_ref.refs_3_.refs_4_), channel_id=1, source_target_pairs={{0,3},{1,2},{2,1},{3,0},{4,7},{5,6},{6,5},{7,4},{8,11},{9,10},{10,... | collective-permute-start | bytes 393224 | tf_op jit(solution)/shard_map/ppermute | solution.py:52
  43.4 4.7 %collective-permute-start.12 = (bf16[64,512]{1,0:T(8,128)(2,1)S(1)}, bf16[64,512]{1,0:T(8,128)(2,1)S(1)}, u32[]{:S(2)}, u32[]{:S(2)}) collective-permute-start(bf16[64,512]{1,0:T(8,128)(2,1)S(1)} %shard_map.73.refs_1_), channel_id=1, source_target_pairs={{0,1},{1,0},{2,3},{3,2},{4,5},{5,4},{6,7},{7,6},{8,9},{9,8},{10,11... | collective-permute-start | bytes 196616 | tf_op jit(solution)/shard_map/ppermute | solution.py:52
  44.2 6.1 %collective-permute-start.10 = (bf16[64,512]{1,0:T(8,128)(2,1)S(1)}, bf16[64,512]{1,0:T(8,128)(2,1)S(1)}, u32[]{:S(2)}, u32[]{:S(2)}) collective-permute-start(bf16[64,512]{1,0:T(8,128)(2,1)S(1)} %shard_map.73.refs_1_), channel_id=1, source_target_pairs={{0,3},{1,2},{2,1},{3,0},{4,7},{5,6},{6,5},{7,4},{8,11},{9,10},{10,... | collective-permute-start | bytes 196616 | tf_op jit(solution)/shard_map/ppermute | solution.py:52
  46.1 5.6 %collective-permute-start.11 = (bf16[64,512]{1,0:T(8,128)(2,1)S(1)}, bf16[64,512]{1,0:T(8,128)(2,1)S(1)}, u32[]{:S(2)}, u32[]{:S(2)}) collective-permute-start(bf16[64,512]{1,0:T(8,128)(2,1)S(1)} %shard_map.73.refs_1_), channel_id=1, source_target_pairs={{0,2},{1,3},{2,0},{3,1},{4,6},{5,7},{6,4},{7,5},{8,10},{9,11},{10,... | collective-permute-start | bytes 196616 | tf_op jit(solution)/shard_map/ppermute | solution.py:52
  52.2 5.0 %collective-permute-start.13 = (bf16[64,1024]{1,0:T(8,128)(2,1)S(1)}, bf16[64,1024]{1,0:T(8,128)(2,1)S(1)}, u32[]{:S(2)}, u32[]{:S(2)}) collective-permute-start(bf16[64,1024]{1,0:T(8,128)(2,1)S(1)} %shard_map.75), channel_id=1, source_target_pairs={{0,4},{1,5},{2,6},{3,7},{4,0},{5,1},{6,2},{7,3},{8,12},{9,13},{10,... | collective-permute-start | bytes 393224 | tf_op jit(solution)/shard_map/ppermute | solution.py:52
  53.7 8.4 %collective-permute-start.16 = (bf16[64,1024]{1,0:T(8,128)(2,1)S(1)}, bf16[64,1024]{1,0:T(8,128)(2,1)S(1)}, u32[]{:S(2)}, u32[]{:S(2)}) collective-permute-start(bf16[64,1024]{1,0:T(8,128)(2,1)S(1)} %shard_map.75), channel_id=1, source_target_pairs={{0,6},{1,7},{2,4},{3,5},{4,2},{5,3},{6,0},{7,1},{8,14},{9,15},{10,... | collective-permute-start | bytes 393224 | tf_op jit(solution)/shard_map/ppermute | solution.py:52
  57.2 5.6 %collective-permute-start.15 = (bf16[64,1024]{1,0:T(8,128)(2,1)S(1)}, bf16[64,1024]{1,0:T(8,128)(2,1)S(1)}, u32[]{:S(2)}, u32[]{:S(2)}) collective-permute-start(bf16[64,1024]{1,0:T(8,128)(2,1)S(1)} %collective-permute-done.13.x_ref.refs_3_.refs_4_), channel_id=1, source_target_pairs={{0,1},{1,0},{2,3},{3,2},{4,5},{5,4},{6,7},{7,6},{8,9},{9,8},{10,11... | collective-permute-start | bytes 393224 | tf_op jit(solution)/shard_map/ppermute | solution.py:52
  57.2 6.9 %collective-permute-start.14 = (bf16[64,1024]{1,0:T(8,128)(2,1)S(1)}, bf16[64,1024]{1,0:T(8,128)(2,1)S(1)}, u32[]{:S(2)}, u32[]{:S(2)}) collective-permute-start(bf16[64,1024]{1,0:T(8,128)(2,1)S(1)} %collective-permute-done.13.x_ref.refs_3_.refs_4_), channel_id=1, source_target_pairs={{0,3},{1,2},{2,1},{3,0},{4,7},{5,6},{6,5},{7,4},{8,11},{9,10},{10,... | collective-permute-start | bytes 393224 | tf_op jit(solution)/shard_map/ppermute | solution.py:52
  65.2 4.4 %collective-permute-start.19 = (bf16[64,512]{1,0:T(8,128)(2,1)S(1)}, bf16[64,512]{1,0:T(8,128)(2,1)S(1)}, u32[]{:S(2)}, u32[]{:S(2)}) collective-permute-start(bf16[64,512]{1,0:T(8,128)(2,1)S(1)} %shard_map.79.refs_1_), channel_id=1, source_target_pairs={{0,1},{1,0},{2,3},{3,2},{4,5},{5,4},{6,7},{7,6},{8,9},{9,8},{10,11... | collective-permute-start | bytes 196616 | tf_op jit(solution)/shard_map/ppermute | solution.py:52
  67.4 6.1 %collective-permute-start.17 = (bf16[64,512]{1,0:T(8,128)(2,1)S(1)}, bf16[64,512]{1,0:T(8,128)(2,1)S(1)}, u32[]{:S(2)}, u32[]{:S(2)}) collective-permute-start(bf16[64,512]{1,0:T(8,128)(2,1)S(1)} %shard_map.79.refs_1_), channel_id=1, source_target_pairs={{0,3},{1,2},{2,1},{3,0},{4,7},{5,6},{6,5},{7,4},{8,11},{9,10},{10,... | collective-permute-start | bytes 196616 | tf_op jit(solution)/shard_map/ppermute | solution.py:52
  69.4 5.4 %collective-permute-start.18 = (bf16[64,512]{1,0:T(8,128)(2,1)S(1)}, bf16[64,512]{1,0:T(8,128)(2,1)S(1)}, u32[]{:S(2)}, u32[]{:S(2)}) collective-permute-start(bf16[64,512]{1,0:T(8,128)(2,1)S(1)} %shard_map.79.refs_1_), channel_id=1, source_target_pairs={{0,2},{1,3},{2,0},{3,1},{4,6},{5,7},{6,4},{7,5},{8,10},{9,11},{10,... | collective-permute-start | bytes 196616 | tf_op jit(solution)/shard_map/ppermute | solution.py:52
